TPU v7x, 32 devices: a whole 2x2x4 slice. The times are simulated.
32 devices in a mesh: row: 8 (over y, x, core), col: 4 (over z).
Axes of the slice: x: 2, y: 2, z: 4, core: 2. Of those that a mesh axis runs over, the one named last changes fastest.
Arguments:
- object_field: float32 [2, 4096, 2048], P(None, 'row', 'col'), may hold values from -6 to 6
- probe: float32 [3, 2, 256, 256], replicated, may hold values from -6 to 6
- raw_counts: bfloat16 [192, 256, 256], P(('row', 'col')), may hold values from 0.099609375 to 10
- resample_delta: float32 [256, 256], replicated, may hold values from -0.1875 to 0.1875
- tile_row: int32 [192, 1], P(('row', 'col')), may hold values from 0 to 7; in each aligned block of 6 rows (0 to 5, 6 to 11, ...) no two rows name the same one
- offsets: int32 [192, 2], P(('row', 'col')), may hold values from 0 to 511
Outputs:
- object_grad: float32 [2, 4096, 2048], P(None, 'row', 'col')
- probe_grad: float32 [3, 2, 256, 256], replicated
Inputs may be any that keep to these rules, and one draw needn't show every extreme that they name: `tile_row`: the 6 frames of one device have distinct tile rows.
All inputs are finite; a program needn't handle non-finite values.
Results may differ from a plain program's by a relative error of at most 0.0008.
The roundings to bfloat16 on the way count: a program that leaves them out, or rounds other values in their place, can miss the bound.
Values may be sent and summed in bfloat16 or wider, within the bound.
A program may use at most 128 MiB of HBM per device.

v0:
```python
import math

import jax
import jax.numpy as jnp
from jax import lax
from jax.experimental import pallas as pl
from jax.experimental.pallas import tpu as pltpu
from jax.sharding import PartitionSpec as P


def extended_2(value, sides, width):
    for axis, dim in sides:
        size, length = (lax.axis_size(axis), value.shape[dim])
        up = [(i, (i + 1) % size) for i in range(size - 1)]
        down = [(j, i) for i, j in up]
        last = lax.slice_in_dim(value, length - width, length, axis=dim)
        first = lax.slice_in_dim(value, 0, width, axis=dim)
        before = lax.ppermute(last, axis, up)
        after = lax.ppermute(first, axis, down)
        value = jnp.concatenate([before, value, after], axis=dim)
    return value


def product(left, right):
    return jnp.dot(left, right, preferred_element_type=jnp.float32)


def dft_tables(points):
    indices = jnp.arange(points, dtype=jnp.int32)
    phases = indices[:, None] * indices[None, :] % points
    angles = phases.astype(jnp.float32) * (2.0 * math.pi / points)
    norming = 1.0 / math.sqrt(points)
    cosine = jnp.cos(angles) * norming
    sine_part = -jnp.sin(angles) * norming
    forward = jnp.concatenate(
        [jnp.concatenate([cosine, -sine_part], 1), jnp.concatenate([sine_part, cosine], 1)], 0
    )
    backward = jnp.concatenate(
        [jnp.concatenate([cosine, sine_part], 1), jnp.concatenate([-sine_part, cosine], 1)], 0
    )
    return (forward.astype(jnp.bfloat16), backward.astype(jnp.bfloat16))


def measure(raw_counts, resample_delta):
    points = resample_delta.shape[0]
    resample = (jnp.eye(points, dtype=jnp.float32) + resample_delta).astype(jnp.bfloat16)
    first = jnp.einsum(
        "ij,kjl->kil", resample, raw_counts, preferred_element_type=jnp.float32
    ).astype(jnp.bfloat16)
    second = jnp.einsum("kij,lj->kil", first, resample, preferred_element_type=jnp.float32)
    return jnp.sqrt(jnp.maximum(second, 0.0)).astype(jnp.bfloat16)


def frames_kernel(
    requests,
    extended,
    probe,
    amplitudes,
    forward,
    backward,
    gradient,
    probe_total,
    window,
    far_field,
):
    mode_count, _, points, _ = probe.shape
    span_rows, span_cols = (points + 8, points + 128)
    gradient[...] = jnp.zeros_like(gradient)
    probe_total[...] = jnp.zeros_like(probe_total)

    def one_slot(slot, carry):
        @pl.when(requests[slot, 2] > 0)
        def _():
            top, left = (requests[slot, 0], requests[slot, 1])
            skip_rows, skip_cols = (lax.rem(top, 8), lax.rem(left, 128))
            rows = pl.ds(pl.multiple_of(top - skip_rows, 8), span_rows)
            cols = pl.ds(pl.multiple_of(left - skip_cols, 128), span_cols)
            for part in range(2):
                block = extended[part, rows, cols]
                block = pltpu.roll(block, lax.rem(span_cols - skip_cols, span_cols), 1)
                block = block[:, :points]
                block = pltpu.roll(block, lax.rem(span_rows - skip_rows, span_rows), 0)
                window[part] = block[:points]
            intensity = jnp.zeros((points, points), jnp.float32)
            for mode in range(mode_count):
                object_real, object_imag = (window[0], window[1])
                probe_real, probe_imag = (probe[mode, 0], probe[mode, 1])
                wave = jnp.concatenate(
                    [
                        (probe_real * object_real - probe_imag * object_imag).astype(jnp.bfloat16),
                        (probe_real * object_imag + probe_imag * object_real).astype(jnp.bfloat16),
                    ],
                    0,
                )
                half_done = product(forward[...], wave).astype(jnp.bfloat16)
                wave_rows = jnp.concatenate([half_done[:points], half_done[points:]], 1)
                field = product(wave_rows, backward[...])
                far_field[mode] = field
                squares = field * field
                intensity = intensity + squares[:, :points] + squares[:, points:]
            amplitude = amplitudes[slot].astype(jnp.float32)
            scaling = 1.0 - amplitude / jnp.sqrt(jnp.maximum(intensity, 1.0))
            scaling = jnp.concatenate([scaling, scaling], 1)
            term_real = jnp.zeros((points, points), jnp.float32)
            term_imag = jnp.zeros((points, points), jnp.float32)
            for mode in range(mode_count):
                residual = (far_field[mode] * scaling).astype(jnp.bfloat16)
                back_rows = product(residual, forward[...]).astype(jnp.bfloat16)
                back_cols = jnp.concatenate([back_rows[:, :points], back_rows[:, points:]], 0)
                update = product(backward[...], back_cols)
                update_real, update_imag = (update[:points], update[points:])
                object_real, object_imag = (window[0], window[1])
                probe_real, probe_imag = (probe[mode, 0], probe[mode, 1])
                term_real = term_real + (probe_real * update_real + probe_imag * update_imag)
                term_imag = term_imag + (probe_real * update_imag - probe_imag * update_real)
                probe_total[mode, 0] += object_real * update_real + object_imag * update_imag
                probe_total[mode, 1] += object_real * update_imag - object_imag * update_real
            for part, term in enumerate((term_real, term_imag)):
                block = jnp.concatenate([term, jnp.zeros((8, points), jnp.float32)], 0)
                block = pltpu.roll(block, skip_rows, 0)
                block = jnp.concatenate([block, jnp.zeros((span_rows, 128), jnp.float32)], 1)
                block = pltpu.roll(block, skip_cols, 1)
                gradient[part, rows, cols] += block

        return carry

    lax.fori_loop(0, requests.shape[0], one_slot, 0)


def frames(requests, extended, probe, amplitudes, forward, backward):
    points = probe.shape[-1]
    vmem = pl.BlockSpec(memory_space=pltpu.VMEM)
    return pl.pallas_call(
        frames_kernel,
        name="frames",
        out_shape=(
            jax.ShapeDtypeStruct(extended.shape, jnp.float32),
            jax.ShapeDtypeStruct(probe.shape, jnp.float32),
        ),
        in_specs=[pl.BlockSpec(memory_space=pltpu.SMEM)] + [vmem] * 5,
        out_specs=(vmem, vmem),
        scratch_shapes=[
            pltpu.VMEM((2, points, points), jnp.float32),
            pltpu.VMEM((probe.shape[0], points, 2 * points), jnp.float32),
        ],
        compiler_params=pltpu.CompilerParams(vmem_limit_bytes=48 * 1024 * 1024),
    )(requests, extended, probe, amplitudes, forward, backward)


def fold(folded, width, tile):
    pieces = ((0, width, 0), (2 * width, tile, 0), (tile + 3 * width, width, tile - width))
    result = jnp.zeros((folded.shape[0], tile, tile), jnp.float32)
    for source_row, length_row, target_row in pieces:
        for source_col, length_col, target_col in pieces:
            block = folded[
                :, source_row : source_row + length_row, source_col : source_col + length_col
            ]
            result = result.at[
                :, target_row : target_row + length_row, target_col : target_col + length_col
            ].add(block)
    return result


def shards(object_field, probe, raw_counts, resample_delta, tile_row, offsets):
    points = probe.shape[-1]
    half = points // 2
    tile = object_field.shape[1]
    tile_rows = lax.axis_size("row")
    frame_total = raw_counts.shape[0] * tile_rows * lax.axis_size("col")
    forward, backward = dft_tables(points)
    amplitudes = measure(raw_counts, resample_delta)
    extended = extended_2(object_field, (("row", 1), ("col", 2)), half)
    slot_ids = jnp.arange(tile_rows, dtype=jnp.int32)
    target = tile_row[:, 0]
    picks = (target[:, None] == slot_ids[None, :]).astype(jnp.int32)
    live = jnp.sum(picks, 0)
    slot_tops = jnp.sum(picks * offsets[:, 0:1], 0)
    slot_lefts = jnp.sum(picks * offsets[:, 1:2], 0)
    requests = jnp.stack([slot_tops, slot_lefts, live], 1)
    outgoing = jnp.einsum(
        "ks,kij->sij", picks.astype(jnp.bfloat16), amplitudes, preferred_element_type=jnp.float32
    ).astype(jnp.bfloat16)
    incoming, received = (
        lax.all_to_all(outgoing, "row", split_axis=0, concat_axis=0, tiled=True),
        lax.all_to_all(requests, "row", split_axis=0, concat_axis=0, tiled=True),
    )

    gradient, probe_total = frames(received, extended, probe, incoming, forward, backward)
    probe_grad = lax.psum(probe_total, ("row", "col")) * (1.0 / math.sqrt(frame_total))
    folded = extended_2(gradient, (("row", 1), ("col", 2)), half)
    object_grad = fold(folded, half, tile)
    return (object_grad, probe_grad)


def solution(mesh):
    placed = (
        P(None, "row", "col"),
        P(),
        P(("row", "col"), None, None),
        P(),
        P(("row", "col"), None),
        P(("row", "col"), None),
    )
    return jax.shard_map(
        shards, mesh=mesh, in_specs=placed, out_specs=(P(None, "row", "col"), P()), check_vma=False
    )
```

profile of v0, /device:TPU:0, one launch (start us, length us, event | category | flops | bytes accessed | tf_op | source)
XLA Modules:
  0.0 263.8 jit_solution(2127038452771969006)
XLA Ops:
  7.2 0.8 slice_bitcast_fusion
  8.0 0.8 select_reduce_fusion.1
  8.8 0.7 copy.10
  9.5 5.2 %all-to-all-start = ((s32[8,1,3]{2,1,0:T(1,128)}), s32[8,1,3]{2,1,0:T(1,128)S(1)}, u32[]{:S(2)}, u32[]{:S(2)}) async-start(s32[8,1,3]{2,1,0:T(1,128)} %copy.10), calls=%async_computation | async-start | bytes 8192 | tf_op jit(solution)/shard_map/all_to_all | solution.py:185
  14.7 1.3 fusion.34
  16.0 2.4 collective-permute-start
  18.4 1.3 collective-permute-start.1
  19.7 0.4 fusion.25
  20.1 0.5 copy.31
  20.6 0.4 fusion.6
  21.1 1.1 copy-done.4
  22.2 0.2 constant_dynamic-update-slice_fusion.1
  22.4 1.0 collective-permute-done.1
  23.4 1.4 fusion.33
  24.8 4.4 %collective-permute-start.2 = (f32[2,768,128]{2,1,0:T(8,128)}, f32[2,768,128]{2,1,0:T(8,128)}, u32[]{:S(2)}, u32[]{:S(2)}) collective-permute-start(f32[2,768,128]{2,1,0:T(8,128)} %get-tuple-element.129), channel_id=1, source_target_pairs={{0,1},{1,2},{2,3},{4,5},{5,6},{6,7},{8,9},{9,10},{10,11},{12,13},{... | collective-permute-start | bytes 2359304 | tf_op jit(solution)/shard_map/ppermute | solution.py:18
  29.2 1.3 collective-permute-start.3
  30.5 1.2 fusion.3
  31.7 1.2 copy.30
  32.8 12.1 %all-to-all-start.1 = ((bf16[8,256,256]{2,1,0:T(8,128)(2,1)}), bf16[8,256,256]{2,1,0:T(8,128)(2,1)S(1)}, u32[]{:S(2)}, u32[]{:S(2)}) async-start(bf16[8,256,256]{2,1,0:T(8,128)(2,1)} %copy.30), calls=%async_computation.1 | async-start | bytes 2097152 | tf_op jit(solution)/shard_map/all_to_all | solution.py:184
  45.0 1.0 fusion.20
  46.0 1.1 negate_convert_fusion
  47.2 4.8 %pad_maximum_fusion.extended = f32[2,768,768]{2,1,0:T(8,128)} fusion(f32[2,768,128]{2,1,0:T(8,128)} %collective-permute-done.3, f32[2,768,512]{2,1,0:T(8,128)} %copy-done.2, f32[2,768,128]{2,1,0:T(8,128)} %collective-permute-done.2), kind=kLoop, calls=%fused_computation | loop fusion | flops 2359296 | bytes 9437184 | tf_op jit(solution)/shard_map/concatenate | solution.py:20
  52.1 8.3 %all-to-all-done.1.amplitudes = bf16[8,256,256]{2,1,0:T(8,128)(2,1)S(1)} async-done(((bf16[8,256,256]{2,1,0:T(8,128)(2,1)}), bf16[8,256,256]{2,1,0:T(8,128)(2,1)S(1)}, u32[]{:S(2)}, u32[]{:S(2)}) %all-to-all-start.1) | async-done | bytes 1048608 | tf_op jit(solution)/shard_map/all_to_all | solution.py:184
  60.3 1.4 copy-done.1
  61.7 26.8 %frames.1 = (f32[2,768,768]{2,1,0:T(8,128)}, f32[3,2,256,256]{3,2,1,0:T(8,128)}) custom-call(s32[8,3]{1,0:T(8,128)S(1)} %bitcast.24, f32[2,768,768]{2,1,0:T(8,128)} %pad_maximum_fusion.extended, f32[3,2,256,256]{3,2,1,0:T(8,128)S(1)} %copy-done.1, bf16[8,256,256]{2,1,0:T(8,128)(2,1)S(1)} %all-to-all-done.1.amplitudes, ...), custom_call_target="tpu_custom_call" | custom-call | tf_op jit(solution)/shard_map/frames/pallas_call | solution.py:133
  88.6 2.4 fusion.32
  90.9 1.3 collective-permute-start.4
  92.3 1.3 collective-permute-start.5
  93.6 0.7 collective-permute-done.4
  94.4 2.9 %constant_dynamic-update-slice_fusion.4 = f32[2,1024,768]{2,1,0:T(8,128)S(1)} fusion(f32[2,1024,768]{2,1,0:T(8,128)S(1)} %constant_dynamic-update-slice_fusion.5, f32[2,768,768]{2,1,0:T(8,128)} %get-tuple-element.120), kind=kLoop, calls=%fused_computation.53 | loop fusion | bytes 9437184
  97.3 8.5 %collective-permute-done.5 = f32[2,128,768]{2,1,0:T(8,128)S(1)} collective-permute-done((f32[2,128,768]{2,1,0:T(8,128)S(1)}, f32[2,128,768]{2,1,0:T(8,128)S(1)}, u32[]{:S(2)}, u32[]{:S(2)}) %collective-permute-start.5) | collective-permute-done | bytes 786464 | tf_op jit(solution)/shard_map/ppermute | solution.py:19
  105.8 1.2 fusion.31
  107.0 2.3 collective-permute-start.6
  109.3 1.3 collective-permute-start.7
  110.6 0.6 fusion.35
  111.2 0.7 and_reduce_fusion
  111.9 127.7 %all-reduce.3.cloned.1.call-done = f32[3,2,256,256]{3,2,1,0:T(8,128)} async-done(((f32[3,2,256,256]{3,2,1,0:T(8,128)}), f32[3,2,256,256]{3,2,1,0:T(8,128)}) %all-reduce.3.cloned.1.call-update) | async-done | bytes 1572880 | tf_op jit(solution)/shard_map/psum | solution.py:189
  239.6 2.8 %broadcast_multiply_fusion = f32[3,2,256,256]{3,2,1,0:T(8,128)} fusion(f32[3,2,256,256]{3,2,1,0:T(8,128)} %all-reduce.3.cloned.1.call-done), kind=kLoop, calls=%fused_computation.13 | loop fusion | flops 393216 | bytes 3145728 | tf_op jit(solution)/shard_map/mul | solution.py:189
  242.4 0.9 slice.317
  243.3 0.3 scatter-add.26
  243.7 2.9 %add_select_fusion.1 = f32[2,128,128]{2,1,0:T(8,128)S(1)} fusion(f32[2,1024,128]{2,1,0:T(8,128)} %collective-permute-done.7, f32[2,512,512]{2,1,0:T(8,128)S(1)} %fusion.11, s32[]{:T(128)} %bitcast.11, s32[]{:T(128)} %bitcast.12, pred[]{:T(512)} %and_reduce_fusion), kind=kLoop, calls=%fused_computation.42 | loop fusion | flops 65536 | bytes 393225 | tf_op jit(solution)/shard_map/select.11
  246.6 2.5 scatter-add.30
  249.1 1.2 fusion.13
  250.3 2.1 slice_add_fusion
  252.4 1.2 fusion.12
  253.6 0.9 fusion.23
  254.7 0.9 fusion.22
  255.7 1.3 copy-done.3
  (39 shorter events, 0.6 us)
Async XLA Ops:
  7.2 12.6 %copy-start = (bf16[6,256,256]{2,1,0:T(8,128)(2,1)S(1)}, bf16[6,256,256]{2,1,0:T(8,128)(2,1)}, u32[]{:S(2)}) copy-start(bf16[6,256,256]{2,1,0:T(8,128)(2,1)} %param.28) | copy-start | bytes 2359300
  7.2 12.6 %copy-start.9 = (f32[256,256]{1,0:T(8,128)S(1)}, f32[256,256]{1,0:T(8,128)}, u32[]{:S(2)}) copy-start(f32[256,256]{1,0:T(8,128)} %param.29) | copy-start | bytes 786436
  9.5 23.4 %all-to-all-start = ((s32[8,1,3]{2,1,0:T(1,128)}), s32[8,1,3]{2,1,0:T(1,128)S(1)}, u32[]{:S(2)}, u32[]{:S(2)}) async-start(s32[8,1,3]{2,1,0:T(1,128)} %copy.10), calls=%async_computation | async-start | bytes 8192 | tf_op jit(solution)/shard_map/all_to_all | solution.py:185
  16.0 5.1 %collective-permute-start = (f32[2,128,512]{2,1,0:T(8,128)S(1)}, f32[2,128,512]{2,1,0:T(8,128)S(1)}, u32[]{:S(2)}, u32[]{:S(2)}) collective-permute-start(f32[2,128,512]{2,1,0:T(8,128)S(1)} %get-tuple-element.132), channel_id=1, source_target_pairs={{0,4},{4,8},{8,12},{12,16},{16,20},{20,24},{24,28},{1,5},{5,9},{9,... | collective-permute-start | bytes 1572872 | tf_op jit(solution)/shard_map/ppermute | solution.py:18
  18.4 4.9 %collective-permute-start.1 = (f32[2,128,512]{2,1,0:T(8,128)S(1)}, f32[2,128,512]{2,1,0:T(8,128)S(1)}, u32[]{:S(2)}, u32[]{:S(2)}) collective-permute-start(f32[2,128,512]{2,1,0:T(8,128)S(1)} %get-tuple-element.131), channel_id=1, source_target_pairs={{4,0},{8,4},{12,8},{16,12},{20,16},{24,20},{28,24},{5,1},{9,5},{13... | collective-permute-start | bytes 1572872 | tf_op jit(solution)/shard_map/ppermute | solution.py:19
  20.6 1.6 copy-start.4
  22.3 8.1 %copy-start.10 = (s32[6,1]{0,1:T(1,128)S(1)}, s32[6,1]{0,1:T(1,128)}, u32[]{:S(2)}) copy-start(s32[6,1]{0,1:T(1,128)} %param.30) | copy-start | bytes 76
  23.4 8.3 %copy-start.2 = (f32[2,768,512]{2,1,0:T(8,128)}, f32[2,768,512]{2,1,0:T(8,128)S(1)}, u32[]{:S(2)}) copy-start(f32[2,768,512]{2,1,0:T(8,128)S(1)} %constant_dynamic-update-slice_fusion) | copy-start | bytes 9437188
  24.8 22.4 %collective-permute-start.2 = (f32[2,768,128]{2,1,0:T(8,128)}, f32[2,768,128]{2,1,0:T(8,128)}, u32[]{:S(2)}, u32[]{:S(2)}) collective-permute-start(f32[2,768,128]{2,1,0:T(8,128)} %get-tuple-element.129), channel_id=1, source_target_pairs={{0,1},{1,2},{2,3},{4,5},{5,6},{6,7},{8,9},{9,10},{10,11},{12,13},{... | collective-permute-start | bytes 2359304 | tf_op jit(solution)/shard_map/ppermute | solution.py:18
  29.2 18.1 %collective-permute-start.3 = (f32[2,768,128]{2,1,0:T(8,128)}, f32[2,768,128]{2,1,0:T(8,128)}, u32[]{:S(2)}, u32[]{:S(2)}) collective-permute-start(f32[2,768,128]{2,1,0:T(8,128)} %get-tuple-element.130), channel_id=1, source_target_pairs={{1,0},{2,1},{3,2},{5,4},{6,5},{7,6},{9,8},{10,9},{11,10},{13,12},{... | collective-permute-start | bytes 2359304 | tf_op jit(solution)/shard_map/ppermute | solution.py:19
  32.8 27.5 %all-to-all-start.1 = ((bf16[8,256,256]{2,1,0:T(8,128)(2,1)}), bf16[8,256,256]{2,1,0:T(8,128)(2,1)S(1)}, u32[]{:S(2)}, u32[]{:S(2)}) async-start(bf16[8,256,256]{2,1,0:T(8,128)(2,1)} %copy.30), calls=%async_computation.1 | async-start | bytes 2097152 | tf_op jit(solution)/shard_map/all_to_all | solution.py:184
  45.0 194.6 %all-reduce.3.cloned.1.call-start = ((), (), s32[]{:S(2)}) async-start(), calls=%async_computation.2 | async-start | bytes 3145728 | tf_op jit(solution)/shard_map/psum | solution.py:189
  60.3 1.4 copy-start.1
  90.9 3.4 %collective-permute-start.4 = (f32[2,128,768]{2,1,0:T(8,128)}, f32[2,128,768]{2,1,0:T(8,128)S(1)}, u32[]{:S(2)}, u32[]{:S(2)}) collective-permute-start(f32[2,128,768]{2,1,0:T(8,128)} %get-tuple-element.128), channel_id=1, source_target_pairs={{0,4},{4,8},{8,12},{12,16},{16,20},{20,24},{24,28},{1,5},{5,9},{9,... | collective-permute-start | bytes 2359304 | tf_op jit(solution)/shard_map/ppermute | solution.py:18
  92.3 13.5 %collective-permute-start.5 = (f32[2,128,768]{2,1,0:T(8,128)S(1)}, f32[2,128,768]{2,1,0:T(8,128)S(1)}, u32[]{:S(2)}, u32[]{:S(2)}) collective-permute-start(f32[2,128,768]{2,1,0:T(8,128)S(1)} %get-tuple-element.127), channel_id=1, source_target_pairs={{4,0},{8,4},{12,8},{16,12},{20,16},{24,20},{28,24},{5,1},{9,5},{13... | collective-permute-start | bytes 2359304 | tf_op jit(solution)/shard_map/ppermute | solution.py:19
  94.3 2.9 %copy-start.7 = (f32[2,128,768]{2,1,0:T(8,128)}, f32[2,128,768]{2,1,0:T(8,128)S(1)}, u32[]{:S(2)}) copy-start(f32[2,128,768]{2,1,0:T(8,128)S(1)} %collective-permute-done.4) | copy-start | bytes 2359300
  105.7 1.2 copy-start.5
  105.8 5.4 %copy-start.11 = (s32[3]{0:T(128)S(1)}, s32[3]{0:T(128)}, u32[]{:S(2)}) copy-start(s32[3]{0:T(128)} %constant.278.clone.1) | copy-start | bytes 40
  107.0 135.4 %collective-permute-start.6 = (f32[2,1024,128]{2,1,0:T(8,128)S(1)}, f32[2,1024,128]{2,1,0:T(8,128)}, u32[]{:S(2)}, u32[]{:S(2)}) collective-permute-start(f32[2,1024,128]{2,1,0:T(8,128)S(1)} %get-tuple-element.126), channel_id=1, source_target_pairs={{0,1},{1,2},{2,3},{4,5},{5,6},{6,7},{8,9},{9,10},{10,11},{12,13},{... | collective-permute-start | bytes 3145736 | tf_op jit(solution)/shard_map/ppermute | solution.py:18
  109.3 134.4 %collective-permute-start.7 = (f32[2,1024,128]{2,1,0:T(8,128)}, f32[2,1024,128]{2,1,0:T(8,128)}, u32[]{:S(2)}, u32[]{:S(2)}) collective-permute-start(f32[2,1024,128]{2,1,0:T(8,128)} %get-tuple-element.125), channel_id=1, source_target_pairs={{1,0},{2,1},{3,2},{5,4},{6,5},{7,6},{9,8},{10,9},{11,10},{13,12},{... | collective-permute-start | bytes 3145736 | tf_op jit(solution)/shard_map/ppermute | solution.py:19
  239.6 4.0 %copy-start.8 = (f32[2,128,768]{2,1,0:T(8,128)S(1)}, f32[2,128,768]{2,1,0:T(8,128)}, u32[]{:S(2)}) copy-start(f32[2,128,768]{2,1,0:T(8,128)} %copy-done.7) | copy-start | bytes 2359300
  252.4 2.2 copy-start.6
  255.7 1.3 copy-start.3
Sparse Core Ops, SparseCore 0:
  93.7 145.8 all-reduce.2
where the time goes:
time: 263 us; the launch traced here: 264 us
  waiting for transfers between devices  146 us (56%)
  starting transfers between devices  33 us (13%)
  Pallas kernels  26.8 us (10%)
  local copies, waits for them, and re-layouts  20.8 us (8%)
  other arithmetic  20.8 us (8%)
  between operations  14.4 us (5%)
    psum x1, waiting for transfers between devices, shards(): lax.psum(probe_total, ('row', 'col')) * (1.0 / math.sqrt(frame_total))  128 us
    pallas_call x1, Pallas kernels, frames(): pl.pallas_call(frames_kernel, name='frames', out_shape=(jax.ShapeDtypeStr...  26.8 us
    all_to_all x1, starting transfers between devices, shards(): lax.all_to_all(outgoing, 'row', split_axis=0, concat_axis=0, tiled=True)  12.1 us
    ppermute x4, starting transfers between devices, extended_2(): before = lax.ppermute(last, axis, up)  10.5 us
    ppermute x4, waiting for transfers between devices, extended_2(): after = lax.ppermute(first, axis, down)  9.43 us
    all_to_all x1, waiting for transfers between devices, shards(): lax.all_to_all(outgoing, 'row', split_axis=0, concat_axis=0, tiled=True)  8.27 us
    unnamed x28, local copies, waits for them, and re-layouts  7.01 us
    another operation x5, other arithmetic  5.7 us
  transfers between devices with their start and end apart: 11, of which 5 were waited for; matrix products, arithmetic and copies ran while one was open for 9% of the time, Pallas kernels for 0%

commit v1 on v0

--- a/solution.py
+++ b/solution.py
@@ -8,17 +8,495 @@
 from jax.sharding import PartitionSpec as P
 
 
-def extended_2(value, sides, width):
-    for axis, dim in sides:
-        size, length = (lax.axis_size(axis), value.shape[dim])
-        up = [(i, (i + 1) % size) for i in range(size - 1)]
-        down = [(j, i) for i, j in up]
-        last = lax.slice_in_dim(value, length - width, length, axis=dim)
-        first = lax.slice_in_dim(value, 0, width, axis=dim)
-        before = lax.ppermute(last, axis, up)
-        after = lax.ppermute(first, axis, down)
-        value = jnp.concatenate([before, value, after], axis=dim)
-    return value
+MESH = pl.DeviceIdType.MESH
+DIRECTIONS = tuple(
+    (down, across) for down in (-1, 0, 1) for across in (-1, 0, 1) if (down, across) != (0, 0)
+)
+
+
+def place():
+    return (
+        lax.axis_index("row"),
+        lax.axis_index("col"),
+        lax.axis_size("row"),
+        lax.axis_size("col"),
+    )
+
+
+def inside(row, col, rows, cols):
+    return (row >= 0) & (row < rows) & (col >= 0) & (col < cols)
+
+
+def inner_edge(step, tile, half):
+    start, size = {-1: (0, half), 0: (0, tile), 1: (tile - half, half)}[step]
+    return pl.ds(start, size)
+
+
+def outer_edge(step, tile, half):
+    start, size = {-1: (0, half), 0: (half, tile), 1: (half + tile, half)}[step]
+    return pl.ds(start, size)
+
+
+def greet(pair):
+    row, col, rows, cols = place()
+    barrier = pltpu.get_barrier_semaphore()
+    others = [(lax.rem(row + i, rows), col) for i in range(1, rows)]
+    if pair:
+        others += [(row, lax.rem(col + i, cols)) for i in range(1, cols)]
+    else:
+        others += [(row, lax.rem(col + i, cols)) for i in (1, cols - 1)]
+    for down in (1, rows - 1):
+        for across in (1, cols - 1):
+            others.append((lax.rem(row + down, rows), lax.rem(col + across, cols)))
+    for other in others:
+        pl.semaphore_signal(barrier, inc=1, device_id=other, device_id_type=MESH)
+    pl.semaphore_wait(barrier, len(others))
+
+
+def gather_kernel(
+    tile_row,
+    offsets,
+    object_field,
+    raw_counts,
+    delta,
+    extended,
+    incoming,
+    infos,
+    outbox,
+    info_out,
+    halo_send,
+    halo_recv,
+    slot_send,
+    slot_recv,
+    info_send,
+    info_recv,
+    center_sem,
+):
+    row, col, rows, cols = place()
+    tile = object_field.shape[1]
+    points = raw_counts.shape[1]
+    half = points // 2
+    frame_count = raw_counts.shape[0]
+    center = pltpu.make_async_copy(
+        object_field, extended.at[:, pl.ds(half, tile), pl.ds(half, tile)], center_sem
+    )
+    center.start()
+    greet(False)
+
+    def halo(index):
+        down, across = DIRECTIONS[index]
+        return pltpu.make_async_remote_copy(
+            src_ref=object_field.at[
+                :, inner_edge(down, tile, half), inner_edge(across, tile, half)
+            ],
+            dst_ref=extended.at[
+                :, outer_edge(-down, tile, half), outer_edge(-across, tile, half)
+            ],
+            send_sem=halo_send.at[index],
+            recv_sem=halo_recv.at[index],
+            device_id=(row + down, col + across),
+            device_id_type=MESH,
+        )
+
+    for index, (down, across) in enumerate(DIRECTIONS):
+
+        @pl.when(inside(row + down, col + across, rows, cols))
+        def _():
+            halo(index).start()
+
+        @pl.when(jnp.logical_not(inside(row - down, col - across, rows, cols)))
+        def _():
+            where = (slice(None), outer_edge(-down, tile, half), outer_edge(-across, tile, half))
+            extended[where] = jnp.zeros(
+                (2, where[1].size, where[2].size), jnp.float32
+            )
+
+    identity = (
+        lax.broadcasted_iota(jnp.int32, (points, points), 0)
+        == lax.broadcasted_iota(jnp.int32, (points, points), 1)
+    ).astype(jnp.float32)
+    resample = (identity + delta[...]).astype(jnp.bfloat16)
+
+    def slot(step):
+        other = lax.rem(row + step, rows)
+        return (
+            pltpu.make_async_remote_copy(
+                src_ref=outbox.at[step],
+                dst_ref=incoming.at[row],
+                send_sem=slot_send.at[step],
+                recv_sem=slot_recv.at[row],
+                device_id=(other, col),
+                device_id_type=MESH,
+            ),
+            pltpu.make_async_remote_copy(
+                src_ref=info_out.at[step],
+                dst_ref=infos.at[row],
+                send_sem=info_send.at[step],
+                recv_sem=info_recv.at[row],
+                device_id=(other, col),
+                device_id_type=MESH,
+            ),
+        )
+
+    lanes = lax.broadcasted_iota(jnp.int32, (8, 128), 1)
+
+    def fill(step, carry):
+        other = lax.rem(row + step, rows)
+        pick, top, left, live = (jnp.int32(0), jnp.int32(0), jnp.int32(0), jnp.int32(0))
+        for k in range(frame_count):
+            hit = tile_row[k, 0] == other
+            pick = jnp.where(hit, k, pick)
+            top = jnp.where(hit, offsets[k, 0], top)
+            left = jnp.where(hit, offsets[k, 1], left)
+            live = jnp.where(hit, 1, live)
+        info = jnp.where(lanes == 0, top, jnp.where(lanes == 1, left, live))
+        first = product(resample, raw_counts[pick]).astype(jnp.bfloat16)
+        second = lax.dot_general(
+            first, resample, (((1,), (1,)), ((), ())), preferred_element_type=jnp.float32
+        )
+        amplitude = jnp.sqrt(jnp.maximum(second, 0.0)).astype(jnp.bfloat16)
+
+        @pl.when(step == 0)
+        def _():
+            incoming[row] = amplitude
+            infos[row] = info
+
+        @pl.when(step > 0)
+        def _():
+            outbox[step] = amplitude
+            info_out[step] = info
+            for copy in slot(step):
+                copy.start()
+
+        return carry
+
+    lax.fori_loop(0, rows, fill, 0)
+
+    for index, (down, across) in enumerate(DIRECTIONS):
+
+        @pl.when(inside(row - down, col - across, rows, cols))
+        def _():
+            halo(index).wait_recv()
+
+        @pl.when(inside(row + down, col + across, rows, cols))
+        def _():
+            halo(index).wait_send()
+
+    center.wait()
+
+    def finish(step, carry):
+        source = lax.rem(row + step, rows)
+        pltpu.make_async_remote_copy(
+            src_ref=outbox.at[step],
+            dst_ref=incoming.at[source],
+            send_sem=slot_send.at[step],
+            recv_sem=slot_recv.at[source],
+            device_id=(source, col),
+            device_id_type=MESH,
+        ).wait()
+        pltpu.make_async_remote_copy(
+            src_ref=info_out.at[step],
+            dst_ref=infos.at[source],
+            send_sem=info_send.at[step],
+            recv_sem=info_recv.at[source],
+            device_id=(source, col),
+            device_id_type=MESH,
+        ).wait()
+        return carry
+
+    lax.fori_loop(1, rows, finish, 0)
+
+
+def gather(tile_row, offsets, object_field, raw_counts, delta):
+    rows = lax.axis_size("row")
+    points = raw_counts.shape[1]
+    reach = object_field.shape[1] + points
+    vmem = pl.BlockSpec(memory_space=pltpu.VMEM)
+    smem = pl.BlockSpec(memory_space=pltpu.SMEM)
+    dma = pltpu.SemaphoreType.DMA
+    return pl.pallas_call(
+        gather_kernel,
+        name="gather",
+        out_shape=(
+            jax.ShapeDtypeStruct((2, reach, reach), jnp.float32),
+            jax.ShapeDtypeStruct((rows, points, points), jnp.bfloat16),
+            jax.ShapeDtypeStruct((rows, 8, 128), jnp.int32),
+        ),
+        in_specs=[smem, smem, pl.BlockSpec(memory_space=pl.ANY), vmem, vmem],
+        out_specs=(vmem, vmem, vmem),
+        scratch_shapes=[
+            pltpu.VMEM((rows, points, points), jnp.bfloat16),
+            pltpu.VMEM((rows, 8, 128), jnp.int32),
+            dma((8,)),
+            dma((8,)),
+            dma((rows,)),
+            dma((rows,)),
+            dma((rows,)),
+            dma((rows,)),
+            dma,
+        ],
+        compiler_params=pltpu.CompilerParams(
+            collective_id=0, has_side_effects=True, vmem_limit_bytes=40 * 1024 * 1024
+        ),
+    )(tile_row, offsets, object_field, raw_counts, delta)
+
+
+def scatter_kernel(
+    gradient,
+    total,
+    folded,
+    summed,
+    halos_tall,
+    halos_wide,
+    corners,
+    pair_in,
+    pair_sum,
+    chip_in,
+    chip_sum,
+    line_in,
+    line_sum,
+    line_out,
+    chip_out,
+    halo_send,
+    halo_recv,
+    pair_sems,
+    chip_sems,
+    line_sems,
+    back_line_sems,
+    back_chip_sems,
+    back_pair_sems,
+):
+    row, col, rows, cols = place()
+    tile = folded.shape[1]
+    half = (gradient.shape[1] - tile) // 2
+    pieces = pair_in.shape[0]
+    length = pair_in.shape[1]
+    chips = rows // 2
+    core, chip = (lax.rem(row, 2), row // 2)
+    chip_rows = length // chips
+    line_rows = chip_rows // cols
+    lanes = summed.shape[2] // 2
+
+    def own_half():
+        return pl.ds(pl.multiple_of(core * lanes, lanes), lanes)
+
+    def sibling_half():
+        return pl.ds(pl.multiple_of((1 - core) * lanes, lanes), lanes)
+
+    sibling = (row + 1 - 2 * core, col)
+    greet(True)
+
+    def landing(index):
+        down, across = DIRECTIONS[index]
+        if down and across:
+            return corners.at[(down + 1) + (across + 1) // 2]
+        return halos_wide.at[(down + 1) // 2] if down else halos_tall.at[(across + 1) // 2]
+
+    def halo(index):
+        down, across = DIRECTIONS[index]
+        return pltpu.make_async_remote_copy(
+            src_ref=gradient.at[:, outer_edge(down, tile, half), outer_edge(across, tile, half)],
+            dst_ref=landing(index),
+            send_sem=halo_send.at[index],
+            recv_sem=halo_recv.at[index],
+            device_id=(row + down, col + across),
+            device_id_type=MESH,
+        )
+
+    def start_halo(index):
+        down, across = DIRECTIONS[index]
+
+        @pl.when(inside(row + down, col + across, rows, cols))
+        def _():
+            halo(index).start()
+
+    def remote(source, target, sems, index, device):
+        return pltpu.make_async_remote_copy(
+            src_ref=source,
+            dst_ref=target,
+            send_sem=sems.at[0, index],
+            recv_sem=sems.at[1, index],
+            device_id=device,
+            device_id_type=MESH,
+        )
+
+    def pair_copy(piece):
+        return remote(
+            total.at[piece, :, sibling_half()], pair_in.at[piece], pair_sems, piece, sibling
+        )
+
+    def chip_copy(piece, step):
+        other = lax.rem(chip + step, chips)
+        start = pl.multiple_of(other * chip_rows, 8)
+        index = piece * chips + step
+        return remote(
+            pair_sum.at[piece, pl.ds(start, chip_rows)],
+            chip_in.at[index],
+            chip_sems,
+            index,
+            (2 * other + core, col),
+        )
+
+    def line_copy(piece, step):
+        other = lax.rem(col + step, cols)
+        start = pl.multiple_of(other * line_rows, 8)
+        index = piece * cols + step
+        return remote(
+            chip_sum.at[piece, pl.ds(start, line_rows)],
+            line_in.at[index],
+            line_sems,
+            index,
+            (row, other),
+        )
+
+    def back_line_copy(piece, step):
+        other = lax.rem(col + step, cols)
+        start = pl.multiple_of(col * line_rows, 8)
+        return remote(
+            line_sum.at[piece],
+            line_out.at[piece, pl.ds(start, line_rows)],
+            back_line_sems,
+            piece * cols + step,
+            (row, other),
+        )
+
+    def back_chip_copy(piece, step):
+        other = lax.rem(chip + step, chips)
+        start = pl.multiple_of(chip * chip_rows, 8)
+        return remote(
+            line_out.at[piece],
+            chip_out.at[piece, pl.ds(start, chip_rows)],
+            back_chip_sems,
+            piece * chips + step,
+            (2 * other + core, col),
+        )
+
+    def back_pair_copy(piece):
+        return remote(
+            chip_out.at[piece],
+            summed.at[piece, :, own_half()],
+            back_pair_sems,
+            piece,
+            sibling,
+        )
+
+    for piece in range(pieces):
+        pair_copy(piece).start()
+    for index, (down, across) in enumerate(DIRECTIONS):
+        if not down:
+            start_halo(index)
+    for piece in range(pieces):
+        pair_copy(piece).wait_recv()
+        pair_sum[piece] = total[piece, :, own_half()] + pair_in[piece]
+        for step in range(1, chips):
+            chip_copy(piece, step).start()
+    for index, (down, across) in enumerate(DIRECTIONS):
+        if down:
+            start_halo(index)
+    for piece in range(pieces):
+        start = pl.multiple_of(chip * chip_rows, 8)
+        value = pair_sum[piece, pl.ds(start, chip_rows)]
+        for step in range(1, chips):
+            chip_copy(piece, step).wait_recv()
+            value = value + chip_in[piece * chips + step]
+        chip_sum[piece] = value
+        for step in range(1, cols):
+            line_copy(piece, step).start()
+    for piece in range(pieces):
+        start = pl.multiple_of(col * line_rows, 8)
+        value = chip_sum[piece, pl.ds(start, line_rows)]
+        for step in range(1, cols):
+            line_copy(piece, step).wait_recv()
+            value = value + line_in[piece * cols + step]
+        line_sum[piece] = value
+        line_out[piece, pl.ds(start, line_rows)] = value
+        for step in range(1, cols):
+            back_line_copy(piece, step).start()
+    for piece in range(pieces):
+        for step in range(1, cols):
+            back_line_copy(piece, step).wait_recv()
+        start = pl.multiple_of(chip * chip_rows, 8)
+        for step in range(1, chips):
+            back_chip_copy(piece, step).start()
+        chip_out[piece, pl.ds(start, chip_rows)] = line_out[piece]
+    for piece in range(pieces):
+        for step in range(1, chips):
+            back_chip_copy(piece, step).wait_recv()
+        back_pair_copy(piece).start()
+        summed[piece, :, own_half()] = chip_out[piece]
+
+    folded[...] = gradient[:, half : half + tile, half : half + tile]
+    for index, (down, across) in enumerate(DIRECTIONS):
+
+        @pl.when(inside(row - down, col - across, rows, cols))
+        def _():
+            halo(index).wait_recv()
+            where = (slice(None), inner_edge(-down, tile, half), inner_edge(-across, tile, half))
+            folded[where] += landing(index)[...]
+
+    for piece in range(pieces):
+        back_pair_copy(piece).wait_recv()
+    for index, (down, across) in enumerate(DIRECTIONS):
+
+        @pl.when(inside(row + down, col + across, rows, cols))
+        def _():
+            halo(index).wait_send()
+
+    for piece in range(pieces):
+        pair_copy(piece).wait_send()
+        back_pair_copy(piece).wait_send()
+        for step in range(1, chips):
+            chip_copy(piece, step).wait_send()
+            back_chip_copy(piece, step).wait_send()
+        for step in range(1, cols):
+            line_copy(piece, step).wait_send()
+            back_line_copy(piece, step).wait_send()
+
+
+def scatter(gradient, total, tile):
+    rows, cols = (lax.axis_size("row"), lax.axis_size("col"))
+    half = (gradient.shape[1] - tile) // 2
+    pieces, _, points, _ = total.shape
+    length, lanes = (2 * points, points // 2)
+    chips = rows // 2
+    f32 = jnp.float32
+    vmem = pl.BlockSpec(memory_space=pltpu.VMEM)
+    dma = pltpu.SemaphoreType.DMA
+    folded, summed = pl.pallas_call(
+        scatter_kernel,
+        name="scatter",
+        out_shape=(
+            jax.ShapeDtypeStruct((2, tile, tile), f32),
+            jax.ShapeDtypeStruct((pieces, length, points), f32),
+        ),
+        in_specs=[vmem, vmem],
+        out_specs=(vmem, vmem),
+        scratch_shapes=[
+            pltpu.VMEM((2, 2, tile, half), f32),
+            pltpu.VMEM((2, 2, half, tile), f32),
+            pltpu.VMEM((4, 2, half, half), f32),
+            pltpu.VMEM((pieces, length, lanes), f32),
+            pltpu.VMEM((pieces, length, lanes), f32),
+            pltpu.VMEM((pieces * chips, length // chips, lanes), f32),
+            pltpu.VMEM((pieces, length // chips, lanes), f32),
+            pltpu.VMEM((pieces * cols, length // chips // cols, lanes), f32),
+            pltpu.VMEM((pieces, length // chips // cols, lanes), f32),
+            pltpu.VMEM((pieces, length // chips, lanes), f32),
+            pltpu.VMEM((pieces, length, lanes), f32),
+            dma((8,)),
+            dma((8,)),
+            dma((2, pieces)),
+            dma((2, pieces * chips)),
+            dma((2, pieces * cols)),
+            dma((2, pieces * cols)),
+            dma((2, pieces * chips)),
+            dma((2, pieces)),
+        ],
+        compiler_params=pltpu.CompilerParams(
+            collective_id=1, has_side_effects=True, vmem_limit_bytes=40 * 1024 * 1024
+        ),
+    )(gradient, total.reshape(pieces, length, points))
+    return folded, summed.reshape(total.shape)
 
 
 def product(left, right):
@@ -39,16 +517,6 @@
         [jnp.concatenate([cosine, sine_part], 1), jnp.concatenate([-sine_part, cosine], 1)], 0
     )
     return (forward.astype(jnp.bfloat16), backward.astype(jnp.bfloat16))
-
-
-def measure(raw_counts, resample_delta):
-    points = resample_delta.shape[0]
-    resample = (jnp.eye(points, dtype=jnp.float32) + resample_delta).astype(jnp.bfloat16)
-    first = jnp.einsum(
-        "ij,kjl->kil", resample, raw_counts, preferred_element_type=jnp.float32
-    ).astype(jnp.bfloat16)
-    second = jnp.einsum("kij,lj->kil", first, resample, preferred_element_type=jnp.float32)
-    return jnp.sqrt(jnp.maximum(second, 0.0)).astype(jnp.bfloat16)
 
 
 def frames_kernel(
@@ -147,49 +615,18 @@
     )(requests, extended, probe, amplitudes, forward, backward)
 
 
-def fold(folded, width, tile):
-    pieces = ((0, width, 0), (2 * width, tile, 0), (tile + 3 * width, width, tile - width))
-    result = jnp.zeros((folded.shape[0], tile, tile), jnp.float32)
-    for source_row, length_row, target_row in pieces:
-        for source_col, length_col, target_col in pieces:
-            block = folded[
-                :, source_row : source_row + length_row, source_col : source_col + length_col
-            ]
-            result = result.at[
-                :, target_row : target_row + length_row, target_col : target_col + length_col
-            ].add(block)
-    return result
-
-
 def shards(object_field, probe, raw_counts, resample_delta, tile_row, offsets):
     points = probe.shape[-1]
-    half = points // 2
     tile = object_field.shape[1]
-    tile_rows = lax.axis_size("row")
-    frame_total = raw_counts.shape[0] * tile_rows * lax.axis_size("col")
+    frame_total = raw_counts.shape[0] * lax.axis_size("row") * lax.axis_size("col")
     forward, backward = dft_tables(points)
-    amplitudes = measure(raw_counts, resample_delta)
-    extended = extended_2(object_field, (("row", 1), ("col", 2)), half)
-    slot_ids = jnp.arange(tile_rows, dtype=jnp.int32)
-    target = tile_row[:, 0]
-    picks = (target[:, None] == slot_ids[None, :]).astype(jnp.int32)
-    live = jnp.sum(picks, 0)
-    slot_tops = jnp.sum(picks * offsets[:, 0:1], 0)
-    slot_lefts = jnp.sum(picks * offsets[:, 1:2], 0)
-    requests = jnp.stack([slot_tops, slot_lefts, live], 1)
-    outgoing = jnp.einsum(
-        "ks,kij->sij", picks.astype(jnp.bfloat16), amplitudes, preferred_element_type=jnp.float32
-    ).astype(jnp.bfloat16)
-    incoming, received = (
-        lax.all_to_all(outgoing, "row", split_axis=0, concat_axis=0, tiled=True),
-        lax.all_to_all(requests, "row", split_axis=0, concat_axis=0, tiled=True),
+    extended, incoming, infos = gather(
+        tile_row, offsets, object_field, raw_counts, resample_delta
     )
-
-    gradient, probe_total = frames(received, extended, probe, incoming, forward, backward)
-    probe_grad = lax.psum(probe_total, ("row", "col")) * (1.0 / math.sqrt(frame_total))
-    folded = extended_2(gradient, (("row", 1), ("col", 2)), half)
-    object_grad = fold(folded, half, tile)
-    return (object_grad, probe_grad)
+    requests = infos[:, 0, :3]
+    gradient, probe_total = frames(requests, extended, probe, incoming, forward, backward)
+    object_grad, summed = scatter(gradient, probe_total, tile)
+    return (object_grad, summed * (1.0 / math.sqrt(frame_total)))
 
 
 def solution(mesh):

time: 263 us -> 121 us (0.46); the launches traced: 264 us -> 119 us
  waiting for transfers between devices: 146 us -> 0 us
  Pallas kernels: 26.8 us -> 106 us
  starting transfers between devices: 33 us -> 0 us
  other arithmetic: 20.8 us -> 3.45 us
  between operations: 14.4 us -> 0.72 us
  local copies, waits for them, and re-layouts: 20.8 us -> 8.98 us
    psum x1 -> x0, waiting for transfers between devices: 128 us -> none  [shards(): lax.psum(probe_total, ('row', 'col')) * (1.0 / math.sqrt(frame_total))]
    pallas_call x0 -> x2, Pallas kernels: none -> 81.9 us  [the longest x1 50 us: scatter(): pl.pallas_call(scatter_kernel, name='scatter', out_shape=(jax.ShapeDtypeS...]
    all_to_all x2 -> x0, starting transfers between devices: 17.3 us -> none  [the longest x1 12.1 us: shards(): lax.all_to_all(outgoing, 'row', split_axis=0, concat_axis=0, tiled=True)]
    ppermute x8 -> x0, starting transfers between devices: 15.6 us -> none  [the longest x4 10.5 us: extended_2(): before = lax.ppermute(last, axis, up)]
    ppermute x8 -> x0, waiting for transfers between devices: 10.2 us -> none  [the longest x4 9.43 us: extended_2(): after = lax.ppermute(first, axis, down)]
    all_to_all x2 -> x0, waiting for transfers between devices: 8.27 us -> none  [the longest x1 8.27 us: shards(): lax.all_to_all(outgoing, 'row', split_axis=0, concat_axis=0, tiled=True)]
    slice x5 -> x1, local copies, waits for them, and re-layouts: 7.17 us -> 0.01 us  [shards(): requests = infos[:, 0, :3]]
    concatenate x1 -> x0, other arithmetic: 4.85 us -> none  [extended_2(): value = jnp.concatenate([before, value, after], axis=dim)]
  transfers between devices with their start and end apart: 11 -> 0, of which waited for: 5 -> 0; matrix products, arithmetic and copies ran while one was open for 9% -> 0% of each run, Pallas kernels for 0% -> 0%
where the time goes in v1:
time: 121 us; the launch traced here: 119 us
  Pallas kernels  106 us (88%)
  local copies, waits for them, and re-layouts  8.98 us (7%)
  other arithmetic  3.45 us (3%)
    pallas_call x1, Pallas kernels, scatter(): pl.pallas_call(scatter_kernel, name='scatter', out_shape=(jax.ShapeDtypeS...  50 us
    pallas_call x1, Pallas kernels, gather(): pl.pallas_call(gather_kernel, name='gather', out_shape=(jax.ShapeDtypeStr...  31.9 us
    pallas_call x1, Pallas kernels, frames(): pl.pallas_call(frames_kernel, name='frames', out_shape=(jax.ShapeDtypeStr...  23.6 us
    unnamed x15, local copies, waits for them, and re-layouts  8.98 us

profile of v1, /device:TPU:0, one launch (start us, length us, event | category | flops | bytes accessed | tf_op | source)
XLA Modules:
  0.0 118.7 jit_solution(7116953791299653200)
XLA Ops:
  0.6 0.0 copy-start.5
  0.6 0.0 copy-start.4
  0.7 0.8 copy.8.tile_row
  1.5 0.8 copy.9.offsets
  2.2 1.0 fusion.8
  3.2 1.1 negate_convert_fusion
  4.4 0.1 fusion.1
  4.4 0.0 copy-done.5
  4.4 0.0 copy-done.4
  4.5 0.0 copy-start.2
  4.5 1.6 %copy-done.2 = f32[2,512,512]{2,1,0:T(8,128)S(1)} copy-done((f32[2,512,512]{2,1,0:T(8,128)S(1)}, f32[2,512,512]{2,1,0:T(8,128)}, u32[]{:S(2)}) %copy-start.2) | copy-done | bytes 2097176
  6.0 0.0 copy-start.3
  6.1 31.9 %gather.1 = (f32[2,768,768]{2,1,0:T(8,128)S(1)}, bf16[8,256,256]{2,1,0:T(8,128)(2,1)S(1)}, s32[8,8,128]{2,1,0:T(8,128)S(1)}) custom-call(s32[6,1]{1,0:T(8,128)S(1)} %copy.8.tile_row, s32[6,2]{1,0:T(8,128)S(1)} %copy.9.offsets, f32[2,512,512]{2,1,0:T(8,128)S(1)} %copy-done.2, bf16[6,256,256]{2,1,0:T(8,128)(2,1)S(1)} %copy-done.4, f32[256,256]{1,0:T(8,128)S(1)} %copy-done.5), custom_call_target="tpu_custom_call" | custom-call | tf_op jit(solution)/shard_map/gather/pallas_call | solution.py:217
  37.9 0.0 copy-start.1
  38.0 2.1 %copy-done.1 = f32[2,768,768]{2,1,0:T(8,128)} copy-done((f32[2,768,768]{2,1,0:T(8,128)}, f32[2,768,768]{2,1,0:T(8,128)S(1)}, u32[]{:S(2)}) %copy-start.1) | copy-done | bytes 4718616
  40.1 0.0 copy-done.3
  40.1 23.6 %frames.1 = (f32[2,768,768]{2,1,0:T(8,128)}, f32[3,2,256,256]{3,2,1,0:T(8,128)S(1)}) custom-call(s32[8,3]{1,0:T(8,128)S(1)} %bitcast.4, f32[2,768,768]{2,1,0:T(8,128)} %copy-done.1, f32[3,2,256,256]{3,2,1,0:T(8,128)S(1)} %copy-done.3, bf16[8,256,256]{2,1,0:T(8,128)(2,1)S(1)} %get-tuple-element.11.amplitudes, bf16[512,512]{1,0:T(8,128)(2,1)S(1)} %get-tuple-element.17.forward, ...), custom_call_target="tpu_custom_call" | custom-call | tf_op jit(solution)/shard_map/frames/pallas_call | solution.py:601
  63.7 0.0 copy-start
  63.7 2.3 %copy-done = f32[2,768,768]{2,1,0:T(8,128)S(1)} copy-done((f32[2,768,768]{2,1,0:T(8,128)S(1)}, f32[2,768,768]{2,1,0:T(8,128)}, u32[]{:S(2)}) %copy-start) | copy-done | bytes 4718616
  66.0 50.0 %scatter.1 = (f32[2,512,512]{2,1,0:T(8,128)S(1)}, f32[3,512,256]{2,1,0:T(8,128)S(1)}) custom-call(f32[2,768,768]{2,1,0:T(8,128)S(1)} %copy-done, f32[3,512,256]{2,1,0:T(8,128)S(1)} %bitcast.3), custom_call_target="tpu_custom_call" | custom-call | tf_op jit(solution)/shard_map/scatter/pallas_call | solution.py:465
  116.1 1.3 %broadcast_multiply_fusion = f32[3,512,256]{2,1,0:T(8,128)} fusion(f32[3,512,256]{2,1,0:T(8,128)S(1)} %get-tuple-element.15), kind=kLoop, calls=%fused_computation | loop fusion | flops 393216 | bytes 3145728 | tf_op jit(solution)/shard_map/mul | solution.py:629
  117.3 1.3 %copy.14 = f32[2,512,512]{2,1,0:T(8,128)} copy(f32[2,512,512]{2,1,0:T(8,128)S(1)} %get-tuple-element.22) | data formatting | bytes 4194304
  (1 shorter events, 0.0 us)
Async XLA Ops:
  0.6 3.8 %copy-start.5 = (f32[256,256]{1,0:T(8,128)S(1)}, f32[256,256]{1,0:T(8,128)}, u32[]{:S(2)}) copy-start(f32[256,256]{1,0:T(8,128)} %delta.1) | copy-start | bytes 786436
  0.6 3.8 %copy-start.4 = (bf16[6,256,256]{2,1,0:T(8,128)(2,1)S(1)}, bf16[6,256,256]{2,1,0:T(8,128)(2,1)}, u32[]{:S(2)}) copy-start(bf16[6,256,256]{2,1,0:T(8,128)(2,1)} %raw_counts.1) | copy-start | bytes 2359300
  4.5 1.6 %copy-start.2 = (f32[2,512,512]{2,1,0:T(8,128)S(1)}, f32[2,512,512]{2,1,0:T(8,128)}, u32[]{:S(2)}) copy-start(f32[2,512,512]{2,1,0:T(8,128)} %object_field.1) | copy-start | bytes 6291460
  6.0 34.0 %copy-start.3 = (f32[3,2,256,256]{3,2,1,0:T(8,128)S(1)}, f32[3,2,256,256]{3,2,1,0:T(8,128)}, u32[]{:S(2)}) copy-start(f32[3,2,256,256]{3,2,1,0:T(8,128)} %probe.1) | copy-start | bytes 4718596
  37.9 2.1 %copy-start.1 = (f32[2,768,768]{2,1,0:T(8,128)}, f32[2,768,768]{2,1,0:T(8,128)S(1)}, u32[]{:S(2)}) copy-start(f32[2,768,768]{2,1,0:T(8,128)S(1)} %get-tuple-element.10.extended) | copy-start | bytes 14155780
  63.7 2.3 %copy-start = (f32[2,768,768]{2,1,0:T(8,128)S(1)}, f32[2,768,768]{2,1,0:T(8,128)}, u32[]{:S(2)}) copy-start(f32[2,768,768]{2,1,0:T(8,128)} %get-tuple-element.12.gradient) | copy-start | bytes 14155780

commit v2 on v1

v2 whole, which is shorter than its diff:
```python
import math

import jax
import jax.numpy as jnp
import numpy as np
from jax import lax
from jax.experimental import pallas as pl
from jax.experimental.pallas import tpu as pltpu
from jax.sharding import PartitionSpec as P


MESH = pl.DeviceIdType.MESH
DIRECTIONS = tuple(
    (down, across) for down in (-1, 0, 1) for across in (-1, 0, 1) if (down, across) != (0, 0)
)


def place():
    return (
        lax.axis_index("row"),
        lax.axis_index("col"),
        lax.axis_size("row"),
        lax.axis_size("col"),
    )


def inside(row, col, rows, cols):
    return (row >= 0) & (row < rows) & (col >= 0) & (col < cols)


def inner_edge(step, tile, half):
    start, size = {-1: (0, half), 0: (0, tile), 1: (tile - half, half)}[step]
    return pl.ds(start, size)


def outer_edge(step, tile, half):
    start, size = {-1: (0, half), 0: (half, tile), 1: (half + tile, half)}[step]
    return pl.ds(start, size)


def greet():
    row, col, rows, cols = place()
    barrier = pltpu.get_barrier_semaphore()
    others = [(lax.rem(row + i, rows), col) for i in range(1, rows)]
    others += [(row, lax.rem(col + i, cols)) for i in range(1, cols)]
    for down in (1, rows - 1):
        for across in (1, cols - 1):
            others.append((lax.rem(row + down, rows), lax.rem(col + across, cols)))
    for other in others:
        pl.semaphore_signal(barrier, inc=1, device_id=other, device_id_type=MESH)
    pl.semaphore_wait(barrier, len(others))


def product(left, right):
    return jnp.dot(left, right, preferred_element_type=jnp.float32)


def dft_tables(points):
    indices = np.arange(points)
    angles = (indices[:, None] * indices[None, :] % points) * (2.0 * math.pi / points)
    cosine = np.cos(angles) / math.sqrt(points)
    sine_part = -np.sin(angles) / math.sqrt(points)
    forward = np.block([[cosine, -sine_part], [sine_part, cosine]])
    backward = np.block([[cosine, sine_part], [-sine_part, cosine]])
    return (jnp.asarray(forward, jnp.bfloat16), jnp.asarray(backward, jnp.bfloat16))


def whole_kernel(
    table,
    object_hbm,
    probe_hbm,
    raw_hbm,
    delta_hbm,
    forward_hbm,
    backward_hbm,
    folded,
    summed,
    probe,
    raw,
    delta,
    forward,
    backward,
    extended,
    incoming,
    outbox,
    infos,
    info_out,
    places,
    windows,
    residuals,
    far_field,
    terms,
    total,
    shifted,
    halos_tall,
    halos_wide,
    corners,
    pair_in,
    pair_sum,
    chip_in,
    chip_sum,
    line_in,
    line_sum,
    line_out,
    chip_out,
    local_sems,
    object_send,
    object_recv,
    slot_send,
    slot_recv,
    info_send,
    info_recv,
    halo_send,
    halo_recv,
    pair_sems,
    chip_sems,
    line_sems,
    back_line_sems,
    back_chip_sems,
    back_pair_sems,
):
    row, col, rows, cols = place()
    tile = folded.shape[1]
    points = raw.shape[1]
    half = points // 2
    reach = tile + points
    mode_count = probe.shape[0]
    frame_count = raw.shape[0]
    gradient = extended

    loads = [
        pltpu.make_async_copy(source, target, local_sems.at[i])
        for i, (source, target) in enumerate(
            (
                (raw_hbm, raw),
                (delta_hbm, delta),
                (object_hbm, extended.at[:, pl.ds(half, tile), pl.ds(half, tile)]),
                (probe_hbm, probe),
                (forward_hbm, forward),
                (backward_hbm, backward),
            )
        )
    ]
    for load in loads:
        load.start()
    greet()

    lanes_of = lax.broadcasted_iota(jnp.int32, (8, 128), 1)

    def chosen(other):
        pick, top, left, live = (jnp.int32(0), jnp.int32(0), jnp.int32(0), jnp.int32(0))
        for k in range(frame_count):
            hit = table[k, 0] == other
            pick = jnp.where(hit, k, pick)
            top = jnp.where(hit, table[k, 1], top)
            left = jnp.where(hit, table[k, 2], left)
            live = jnp.where(hit, 1, live)
        return pick, top, left, live

    def info_copy(step, target, other):
        return pltpu.make_async_remote_copy(
            src_ref=info_out.at[step],
            dst_ref=infos.at[target],
            send_sem=info_send.at[step],
            recv_sem=info_recv.at[target],
            device_id=(other, col),
            device_id_type=MESH,
        )

    def slot_copy(step, target, other):
        return pltpu.make_async_remote_copy(
            src_ref=outbox.at[step],
            dst_ref=incoming.at[target],
            send_sem=slot_send.at[step],
            recv_sem=slot_recv.at[target],
            device_id=(other, col),
            device_id_type=MESH,
        )

    def tell(step, carry):
        other = lax.rem(row + step, rows)
        _, top, left, live = chosen(other)
        info = jnp.where(lanes_of == 0, top, jnp.where(lanes_of == 1, left, live))

        @pl.when(step == 0)
        def _():
            infos[row] = info

        @pl.when(step > 0)
        def _():
            info_out[step] = info
            info_copy(step, row, other).start()

        return carry

    lax.fori_loop(0, rows, tell, 0)

    def object_halo(index):
        down, across = DIRECTIONS[index]
        return pltpu.make_async_remote_copy(
            src_ref=object_hbm.at[
                :, inner_edge(down, tile, half), inner_edge(across, tile, half)
            ],
            dst_ref=extended.at[
                :, outer_edge(-down, tile, half), outer_edge(-across, tile, half)
            ],
            send_sem=object_send.at[index],
            recv_sem=object_recv.at[index],
            device_id=(row + down, col + across),
            device_id_type=MESH,
        )

    for index, (down, across) in enumerate(DIRECTIONS):

        @pl.when(inside(row + down, col + across, rows, cols))
        def _():
            object_halo(index).start()

        @pl.when(jnp.logical_not(inside(row - down, col - across, rows, cols)))
        def _():
            where = (slice(None), outer_edge(-down, tile, half), outer_edge(-across, tile, half))
            extended[where] = jnp.zeros((2, where[1].size, where[2].size), jnp.float32)

    loads[0].wait()
    loads[1].wait()
    identity = (
        lax.broadcasted_iota(jnp.int32, (points, points), 0)
        == lax.broadcasted_iota(jnp.int32, (points, points), 1)
    ).astype(jnp.float32)
    resample = (identity + delta[...]).astype(jnp.bfloat16)

    def measure(step, carry):
        other = lax.rem(row + step, rows)
        pick, _, _, _ = chosen(other)
        first = product(resample, raw[pick]).astype(jnp.bfloat16)
        second = lax.dot_general(
            first, resample, (((1,), (1,)), ((), ())), preferred_element_type=jnp.float32
        )
        amplitude = jnp.sqrt(jnp.maximum(second, 0.0)).astype(jnp.bfloat16)

        @pl.when(step == 0)
        def _():
            incoming[row] = amplitude

        @pl.when(step > 0)
        def _():
            outbox[step] = amplitude
            slot_copy(step, row, other).start()

        return carry

    lax.fori_loop(0, rows, measure, 0)

    def heard(step, carry):
        source = lax.rem(row - step + rows, rows)
        info_copy(step, source, source).wait()
        return carry

    lax.fori_loop(1, rows, heard, 0)
    noted = pltpu.make_async_copy(infos, places, local_sems.at[6])
    noted.start()
    total[...] = jnp.zeros_like(total)
    for load in loads[2:]:
        load.wait()
    noted.wait()
    for index, (down, across) in enumerate(DIRECTIONS):

        @pl.when(inside(row - down, col - across, rows, cols))
        def _():
            object_halo(index).wait_recv()

    span_rows, span_cols = (points + 8, points + 128)

    def spot(step):
        source = lax.rem(row - step + rows, rows)
        return source, places[source, 0, 0], places[source, 0, 1], places[source, 0, 2]

    def onward(step, carry):
        source, top, left, live = spot(step)
        skip_rows, skip_cols = (lax.rem(top, 8), lax.rem(left, 128))
        across_rows = pl.ds(lax.div(top, 8) * 8, span_rows)
        across_cols = pl.ds(lax.div(left, 128) * 128, span_cols)
        for part in range(2):
            block = extended[part, across_rows, across_cols]
            block = pltpu.roll(block, lax.rem(span_cols - skip_cols, span_cols), 1)
            block = block[:, :points]
            block = pltpu.roll(block, lax.rem(span_rows - skip_rows, span_rows), 0)
            windows[step, part] = block[:points]
        intensity = jnp.zeros((points, points), jnp.float32)
        for mode in range(mode_count):
            object_real, object_imag = (windows[step, 0], windows[step, 1])
            probe_real, probe_imag = (probe[mode, 0], probe[mode, 1])
            wave = jnp.concatenate(
                [
                    (probe_real * object_real - probe_imag * object_imag).astype(jnp.bfloat16),
                    (probe_real * object_imag + probe_imag * object_real).astype(jnp.bfloat16),
                ],
                0,
            )
            half_done = product(forward[...], wave).astype(jnp.bfloat16)
            wave_rows = jnp.concatenate([half_done[:points], half_done[points:]], 1)
            field = product(wave_rows, backward[...])
            far_field[mode] = field
            squares = field * field
            intensity = intensity + squares[:, :points] + squares[:, points:]

        @pl.when(step > 0)
        def _():
            slot_copy(step, source, source).wait_recv()

        amplitude = incoming[source].astype(jnp.float32)
        scaling = 1.0 - amplitude / jnp.sqrt(jnp.maximum(intensity, 1.0))
        scaling = scaling * live.astype(jnp.float32)
        scaling = jnp.concatenate([scaling, scaling], 1)
        for mode in range(mode_count):
            residuals[step, mode] = (far_field[mode] * scaling).astype(jnp.bfloat16)
        return carry

    lax.fori_loop(0, rows, onward, 0)

    def back(mode):
        def one(step, carry):
            back_rows = product(residuals[step, mode], forward[...]).astype(jnp.bfloat16)
            back_cols = jnp.concatenate([back_rows[:, :points], back_rows[:, points:]], 0)
            update = product(backward[...], back_cols)
            update_real, update_imag = (update[:points], update[points:])
            object_real, object_imag = (windows[step, 0], windows[step, 1])
            probe_real, probe_imag = (probe[mode, 0], probe[mode, 1])
            term_real = probe_real * update_real + probe_imag * update_imag
            term_imag = probe_real * update_imag - probe_imag * update_real
            if mode == 0:
                terms[step, 0] = term_real
                terms[step, 1] = term_imag
            else:
                terms[step, 0] += term_real
                terms[step, 1] += term_imag
            total[mode, :points] += object_real * update_real + object_imag * update_imag
            total[mode, points:] += object_real * update_imag - object_imag * update_real
            return carry

        return one

    def accumulate():
        gradient[...] = jnp.zeros_like(gradient)
        shifted[...] = jnp.zeros_like(shifted)
        chunk = 64

        def one(step, carry):
            _, top, left, _ = spot(step)
            skip_rows = lax.rem(top, 8)
            base = tile // 8 - lax.div(top, 8)
            for part in range(2):
                block = jnp.concatenate(
                    [terms[step, part], jnp.zeros((8, points), jnp.float32)], 0
                )
                block = pltpu.roll(block, skip_rows, 0)
                block = jnp.concatenate(
                    [block, jnp.zeros((span_rows, reach - points), jnp.float32)], 1
                )
                shifted[pl.ds(tile, span_rows)] = pltpu.roll(block, left, 1)

                def add(index, inner):
                    start = pl.multiple_of(index * chunk, 8)
                    source = (base + index * (chunk // 8)) * 8
                    gradient[part, pl.ds(start, chunk)] += shifted[pl.ds(source, chunk)]
                    return inner

                lax.fori_loop(0, reach // chunk, add, 0)
            return carry

        lax.fori_loop(0, rows, one, 0)

    pieces = pair_in.shape[0]
    length = pair_in.shape[1]
    chips = rows // 2
    core, chip = (lax.rem(row, 2), row // 2)
    chip_rows = length // chips
    line_rows = chip_rows // cols
    lanes = summed.shape[2] // 2

    def own_half():
        return pl.ds(pl.multiple_of(core * lanes, lanes), lanes)

    def sibling_half():
        return pl.ds(pl.multiple_of((1 - core) * lanes, lanes), lanes)

    sibling = (row + 1 - 2 * core, col)
    def landing(index):
        down, across = DIRECTIONS[index]
        if down and across:
            return corners.at[(down + 1) + (across + 1) // 2]
        return halos_wide.at[(down + 1) // 2] if down else halos_tall.at[(across + 1) // 2]

    def halo(index):
        down, across = DIRECTIONS[index]
        return pltpu.make_async_remote_copy(
            src_ref=gradient.at[:, outer_edge(down, tile, half), outer_edge(across, tile, half)],
            dst_ref=landing(index),
            send_sem=halo_send.at[index],
            recv_sem=halo_recv.at[index],
            device_id=(row + down, col + across),
            device_id_type=MESH,
        )

    def start_halo(index):
        down, across = DIRECTIONS[index]

        @pl.when(inside(row + down, col + across, rows, cols))
        def _():
            halo(index).start()

    def remote(source, target, sems, index, device):
        return pltpu.make_async_remote_copy(
            src_ref=source,
            dst_ref=target,
            send_sem=sems.at[0, index],
            recv_sem=sems.at[1, index],
            device_id=device,
            device_id_type=MESH,
        )

    def pair_copy(piece):
        return remote(
            total.at[piece, :, sibling_half()], pair_in.at[piece], pair_sems, piece, sibling
        )

    def chip_copy(piece, step):
        other = lax.rem(chip + step, chips)
        start = pl.multiple_of(other * chip_rows, 8)
        index = piece * chips + step
        return remote(
            pair_sum.at[piece, pl.ds(start, chip_rows)],
            chip_in.at[index],
            chip_sems,
            index,
            (2 * other + core, col),
        )

    def line_copy(piece, step):
        other = lax.rem(col + step, cols)
        start = pl.multiple_of(other * line_rows, 8)
        index = piece * cols + step
        return remote(
            chip_sum.at[piece, pl.ds(start, line_rows)],
            line_in.at[index],
            line_sems,
            index,
            (row, other),
        )

    def back_line_copy(piece, step):
        other = lax.rem(col + step, cols)
        start = pl.multiple_of(col * line_rows, 8)
        return remote(
            line_sum.at[piece],
            line_out.at[piece, pl.ds(start, line_rows)],
            back_line_sems,
            piece * cols + step,
            (row, other),
        )

    def back_chip_copy(piece, step):
        other = lax.rem(chip + step, chips)
        start = pl.multiple_of(chip * chip_rows, 8)
        return remote(
            line_out.at[piece],
            chip_out.at[piece, pl.ds(start, chip_rows)],
            back_chip_sems,
            piece * chips + step,
            (2 * other + core, col),
        )

    def back_pair_copy(piece):
        return remote(
            chip_out.at[piece],
            summed.at[piece, :, own_half()],
            back_pair_sems,
            piece,
            sibling,
        )

    def pair_stage(piece):
        pair_copy(piece).wait_recv()
        pair_sum[piece] = total[piece, :, own_half()] + pair_in[piece]
        for step in range(1, chips):
            chip_copy(piece, step).start()

    def chip_stage(piece):
        start = pl.multiple_of(chip * chip_rows, 8)
        value = pair_sum[piece, pl.ds(start, chip_rows)]
        for step in range(1, chips):
            chip_copy(piece, step).wait_recv()
            value = value + chip_in[piece * chips + step]
        chip_sum[piece] = value
        for step in range(1, cols):
            line_copy(piece, step).start()

    def line_stage(piece):
        start = pl.multiple_of(col * line_rows, 8)
        value = chip_sum[piece, pl.ds(start, line_rows)]
        for step in range(1, cols):
            line_copy(piece, step).wait_recv()
            value = value + line_in[piece * cols + step]
        line_sum[piece] = value
        line_out[piece, pl.ds(start, line_rows)] = value
        for step in range(1, cols):
            back_line_copy(piece, step).start()

    def back_line_stage(piece):
        for step in range(1, cols):
            back_line_copy(piece, step).wait_recv()
        start = pl.multiple_of(chip * chip_rows, 8)
        for step in range(1, chips):
            back_chip_copy(piece, step).start()
        chip_out[piece, pl.ds(start, chip_rows)] = line_out[piece]

    def back_chip_stage(piece):
        for step in range(1, chips):
            back_chip_copy(piece, step).wait_recv()
        back_pair_copy(piece).start()
        summed[piece, :, own_half()] = chip_out[piece]

    stages = (pair_stage, chip_stage, line_stage, back_line_stage, back_chip_stage)
    reached = [0] * pieces

    def advance(piece):
        if reached[piece] < len(stages):
            stages[reached[piece]](piece)
            reached[piece] += 1

    middle = rows // 2
    for mode in range(mode_count):
        lax.fori_loop(0, middle, back(mode), 0)
        for piece in range(mode):
            advance(piece)
        lax.fori_loop(middle, rows, back(mode), 0)
        for piece in range(mode - 1):
            advance(piece)
        pair_copy(mode).start()

    for index, (down, across) in enumerate(DIRECTIONS):

        @pl.when(inside(row + down, col + across, rows, cols))
        def _():
            object_halo(index).wait_send()

    accumulate()
    for index, (down, across) in enumerate(DIRECTIONS):
        if not down:
            start_halo(index)
    for piece in range(pieces):
        advance(piece)
    for index, (down, across) in enumerate(DIRECTIONS):
        if down:
            start_halo(index)
    folded[...] = gradient[:, half : half + tile, half : half + tile]
    for _ in stages:
        for piece in range(pieces):
            advance(piece)

    for index, (down, across) in enumerate(DIRECTIONS):

        @pl.when(inside(row - down, col - across, rows, cols))
        def _():
            halo(index).wait_recv()
            where = (slice(None), inner_edge(-down, tile, half), inner_edge(-across, tile, half))
            folded[where] += landing(index)[...]

    for piece in range(pieces):
        back_pair_copy(piece).wait_recv()
    for index, (down, across) in enumerate(DIRECTIONS):

        @pl.when(inside(row + down, col + across, rows, cols))
        def _():
            halo(index).wait_send()

    def sent(step, carry):
        slot_copy(step, row, lax.rem(row + step, rows)).wait_send()
        return carry

    lax.fori_loop(1, rows, sent, 0)
    for piece in range(pieces):
        pair_copy(piece).wait_send()
        back_pair_copy(piece).wait_send()
        for step in range(1, chips):
            chip_copy(piece, step).wait_send()
            back_chip_copy(piece, step).wait_send()
        for step in range(1, cols):
            line_copy(piece, step).wait_send()
            back_line_copy(piece, step).wait_send()


def whole(table, object_field, probe, raw_counts, delta, forward, backward):
    rows, cols = (lax.axis_size("row"), lax.axis_size("col"))
    tile = object_field.shape[1]
    modes, _, points, _ = probe.shape
    half = points // 2
    reach = tile + points
    length, lanes = (2 * points, points // 2)
    chips = rows // 2
    f32, bf16, i32 = (jnp.float32, jnp.bfloat16, jnp.int32)
    vmem = pl.BlockSpec(memory_space=pltpu.VMEM)
    hbm = pl.BlockSpec(memory_space=pl.ANY)
    dma = pltpu.SemaphoreType.DMA
    return pl.pallas_call(
        whole_kernel,
        name="whole",
        out_shape=(
            jax.ShapeDtypeStruct((2, tile, tile), f32),
            jax.ShapeDtypeStruct((modes, length, points), f32),
        ),
        in_specs=[pl.BlockSpec(memory_space=pltpu.SMEM)] + [hbm] * 6,
        out_specs=(vmem, vmem),
        scratch_shapes=[
            pltpu.VMEM(probe.shape, f32),
            pltpu.VMEM(raw_counts.shape, bf16),
            pltpu.VMEM(delta.shape, f32),
            pltpu.VMEM(forward.shape, bf16),
            pltpu.VMEM(backward.shape, bf16),
            pltpu.VMEM((2, reach, reach), f32),
            pltpu.VMEM((rows, points, points), bf16),
            pltpu.VMEM((rows, points, points), bf16),
            pltpu.VMEM((rows, 8, 128), i32),
            pltpu.VMEM((rows, 8, 128), i32),
            pltpu.SMEM((rows, 8, 128), i32),
            pltpu.VMEM((rows, 2, points, points), f32),
            pltpu.VMEM((rows, modes, points, 2 * points), bf16),
            pltpu.VMEM((modes, points, 2 * points), f32),
            pltpu.VMEM((rows, 2, points, points), f32),
            pltpu.VMEM((modes, length, points), f32),
            pltpu.VMEM((2 * tile + points, reach), f32),
            pltpu.VMEM((2, 2, tile, half), f32),
            pltpu.VMEM((2, 2, half, tile), f32),
            pltpu.VMEM((4, 2, half, half), f32),
            pltpu.VMEM((modes, length, lanes), f32),
            pltpu.VMEM((modes, length, lanes), f32),
            pltpu.VMEM((modes * chips, length // chips, lanes), f32),
            pltpu.VMEM((modes, length // chips, lanes), f32),
            pltpu.VMEM((modes * cols, length // chips // cols, lanes), f32),
            pltpu.VMEM((modes, length // chips // cols, lanes), f32),
            pltpu.VMEM((modes, length // chips, lanes), f32),
            pltpu.VMEM((modes, length, lanes), f32),
            dma((7,)),
            dma((8,)),
            dma((8,)),
            dma((rows,)),
            dma((rows,)),
            dma((rows,)),
            dma((rows,)),
            dma((8,)),
            dma((8,)),
            dma((2, modes)),
            dma((2, modes * chips)),
            dma((2, modes * cols)),
            dma((2, modes * cols)),
            dma((2, modes * chips)),
            dma((2, modes)),
        ],
        compiler_params=pltpu.CompilerParams(
            collective_id=0, has_side_effects=True, vmem_limit_bytes=67043328
        ),
    )(table, object_field, probe, raw_counts, delta, forward, backward)


def shards(object_field, probe, raw_counts, resample_delta, tile_row, offsets):
    points = probe.shape[-1]
    frame_total = raw_counts.shape[0] * lax.axis_size("row") * lax.axis_size("col")
    forward, backward = dft_tables(points)
    table = jnp.concatenate([tile_row, offsets], 1)
    object_grad, summed = whole(
        table, object_field, probe, raw_counts, resample_delta, forward, backward
    )
    return (object_grad, summed.reshape(probe.shape) * (1.0 / math.sqrt(frame_total)))


def solution(mesh):
    placed = (
        P(None, "row", "col"),
        P(),
        P(("row", "col"), None, None),
        P(),
        P(("row", "col"), None),
        P(("row", "col"), None),
    )
    return jax.shard_map(
        shards, mesh=mesh, in_specs=placed, out_specs=(P(None, "row", "col"), P()), check_vma=False
    )
```

time: 121 us -> 112 us (0.926); the launches traced: 119 us -> 111 us
  local copies, waits for them, and re-layouts: 8.98 us -> 2.83 us
  Pallas kernels: 106 us -> 104 us
    unnamed x15 -> x5, local copies, waits for them, and re-layouts: 8.98 us -> 2.83 us
    another operation x2 -> x0, other arithmetic: 2.1 us -> none
    mul x1, other arithmetic: 1.28 us -> 2.83 us  [shards(): summed.reshape(probe.shape) * (1.0 / math.sqrt(frame_total))]
    pallas_call x3 -> x1, Pallas kernels: 106 us -> 104 us  [whole(): pl.pallas_call(whole_kernel, name='whole', out_shape=(jax.ShapeDtypeStruc...]
where the time goes in v2:
time: 112 us; the launch traced here: 111 us
  Pallas kernels  104 us (93%)
  other arithmetic  3.5 us (3%)
  local copies, waits for them, and re-layouts  2.83 us (3%)
    pallas_call x1, Pallas kernels, whole(): pl.pallas_call(whole_kernel, name='whole', out_shape=(jax.ShapeDtypeStruc...  104 us
    mul x1, other arithmetic, shards(): summed.reshape(probe.shape) * (1.0 / math.sqrt(frame_total))  2.83 us
    unnamed x5, local copies, waits for them, and re-layouts  2.83 us

profile of v2, /device:TPU:0, one launch (start us, length us, event | category | flops | bytes accessed | tf_op | source)
XLA Modules:
  0.0 111.5 jit_solution(2344268482446933667)
XLA Ops:
  0.6 0.7 copy.10
  1.4 0.8 copy.11
  2.1 0.7 pad_add_fusion.table
  2.8 104.5 %whole.1 = (f32[2,512,512]{2,1,0:T(8,128)}, f32[3,512,256]{2,1,0:T(8,128)}) custom-call(s32[6,3]{1,0:T(8,128)} %pad_add_fusion.table, f32[2,512,512]{2,1,0:T(8,128)} %object_hbm.1, f32[3,2,256,256]{3,2,1,0:T(8,128)} %probe_hbm.1, bf16[6,256,256]{2,1,0:T(8,128)(2,1)} %raw_hbm.1, f32[256,256]{1,0:T(8,128)} %delta_hbm.1, ...), custom_call_target="tpu_custom_call" | custom-call | tf_op jit(solution)/shard_map/whole/pallas_call | solution.py:605
  107.3 0.0 copy-start
  107.3 2.8 %broadcast_multiply_fusion = f32[3,512,256]{2,1,0:T(8,128)} fusion(f32[3,512,256]{2,1,0:T(8,128)} %get-tuple-element.5), kind=kLoop, calls=%fused_computation | loop fusion | flops 393216 | bytes 3145728 | tf_op jit(solution)/shard_map/mul | solution.py:673
  110.2 0.0 copy-done
  110.2 1.3 %copy.13 = f32[2,512,512]{2,1,0:T(8,128)} copy(f32[2,512,512]{2,1,0:T(8,128)S(1)} %copy-done) | data formatting | bytes 4194304
Async XLA Ops:
  107.3 2.8 %copy-start = (f32[2,512,512]{2,1,0:T(8,128)S(1)}, f32[2,512,512]{2,1,0:T(8,128)}, u32[]{:S(2)}) copy-start(f32[2,512,512]{2,1,0:T(8,128)} %get-tuple-element.8) | copy-start | bytes 6291460

commit v3 on v2

--- a/solution.py
+++ b/solution.py
@@ -10,6 +10,7 @@
 
 
 MESH = pl.DeviceIdType.MESH
+GROUP = 2
 DIRECTIONS = tuple(
     (down, across) for down in (-1, 0, 1) for across in (-1, 0, 1) if (down, across) != (0, 0)
 )
@@ -260,6 +261,7 @@
     noted = pltpu.make_async_copy(infos, places, local_sems.at[6])
     noted.start()
     total[...] = jnp.zeros_like(total)
+    shifted[...] = jnp.zeros_like(shifted)
     for load in loads[2:]:
         load.wait()
     noted.wait()
@@ -287,6 +289,7 @@
             block = pltpu.roll(block, lax.rem(span_rows - skip_rows, span_rows), 0)
             windows[step, part] = block[:points]
         intensity = jnp.zeros((points, points), jnp.float32)
+        halves = []
         for mode in range(mode_count):
             object_real, object_imag = (windows[step, 0], windows[step, 1])
             probe_real, probe_imag = (probe[mode, 0], probe[mode, 1])
@@ -297,7 +300,8 @@
                 ],
                 0,
             )
-            half_done = product(forward[...], wave).astype(jnp.bfloat16)
+            halves.append(product(forward[...], wave).astype(jnp.bfloat16))
+        for mode, half_done in enumerate(halves):
             wave_rows = jnp.concatenate([half_done[:points], half_done[points:]], 1)
             field = product(wave_rows, backward[...])
             far_field[mode] = field
@@ -318,57 +322,71 @@
 
     lax.fori_loop(0, rows, onward, 0)
 
-    def back(mode):
-        def one(step, carry):
-            back_rows = product(residuals[step, mode], forward[...]).astype(jnp.bfloat16)
-            back_cols = jnp.concatenate([back_rows[:, :points], back_rows[:, points:]], 0)
-            update = product(backward[...], back_cols)
-            update_real, update_imag = (update[:points], update[points:])
-            object_real, object_imag = (windows[step, 0], windows[step, 1])
-            probe_real, probe_imag = (probe[mode, 0], probe[mode, 1])
-            term_real = probe_real * update_real + probe_imag * update_imag
-            term_imag = probe_real * update_imag - probe_imag * update_real
-            if mode == 0:
-                terms[step, 0] = term_real
-                terms[step, 1] = term_imag
-            else:
-                terms[step, 0] += term_real
-                terms[step, 1] += term_imag
-            total[mode, :points] += object_real * update_real + object_imag * update_imag
-            total[mode, points:] += object_real * update_imag - object_imag * update_real
+    def back(mode, group):
+        def one(index, carry):
+            steps = [index * group + k for k in range(group)]
+            backs = [
+                product(residuals[step, mode], forward[...]).astype(jnp.bfloat16)
+                for step in steps
+            ]
+            updates = [
+                product(
+                    backward[...], jnp.concatenate([rows_[:, :points], rows_[:, points:]], 0)
+                )
+                for rows_ in backs
+            ]
+            sum_real = total[mode, :points]
+            sum_imag = total[mode, points:]
+            for step, update in zip(steps, updates):
+                update_real, update_imag = (update[:points], update[points:])
+                object_real, object_imag = (windows[step, 0], windows[step, 1])
+                probe_real, probe_imag = (probe[mode, 0], probe[mode, 1])
+                term_real = probe_real * update_real + probe_imag * update_imag
+                term_imag = probe_real * update_imag - probe_imag * update_real
+                if mode == 0:
+                    terms[step, 0] = term_real
+                    terms[step, 1] = term_imag
+                else:
+                    terms[step, 0] += term_real
+                    terms[step, 1] += term_imag
+                sum_real = sum_real + (object_real * update_real + object_imag * update_imag)
+                sum_imag = sum_imag + (object_real * update_imag - object_imag * update_real)
+            total[mode, :points] = sum_real
+            total[mode, points:] = sum_imag
             return carry
 
         return one
 
-    def accumulate():
-        gradient[...] = jnp.zeros_like(gradient)
-        shifted[...] = jnp.zeros_like(shifted)
+    def accumulate(begin, end):
         chunk = 64
 
         def one(step, carry):
             _, top, left, _ = spot(step)
-            skip_rows = lax.rem(top, 8)
+            skip_rows, skip_cols = (lax.rem(top, 8), lax.rem(left, 128))
             base = tile // 8 - lax.div(top, 8)
+            across = (tile // 128 - 1 - lax.div(left, 128)) * 128
             for part in range(2):
                 block = jnp.concatenate(
                     [terms[step, part], jnp.zeros((8, points), jnp.float32)], 0
                 )
                 block = pltpu.roll(block, skip_rows, 0)
-                block = jnp.concatenate(
-                    [block, jnp.zeros((span_rows, reach - points), jnp.float32)], 1
+                block = jnp.concatenate([block, jnp.zeros((span_rows, 128), jnp.float32)], 1)
+                shifted[pl.ds(tile, span_rows), pl.ds(tile - 128, span_cols)] = pltpu.roll(
+                    block, skip_cols, 1
                 )
-                shifted[pl.ds(tile, span_rows)] = pltpu.roll(block, left, 1)
 
                 def add(index, inner):
                     start = pl.multiple_of(index * chunk, 8)
                     source = (base + index * (chunk // 8)) * 8
-                    gradient[part, pl.ds(start, chunk)] += shifted[pl.ds(source, chunk)]
+                    gradient[part, pl.ds(start, chunk)] += shifted[
+                        pl.ds(source, chunk), pl.ds(across, reach)
+                    ]
                     return inner
 
                 lax.fori_loop(0, reach // chunk, add, 0)
             return carry
 
-        lax.fori_loop(0, rows, one, 0)
+        lax.fori_loop(begin, end, one, 0)
 
     pieces = pair_in.shape[0]
     length = pair_in.shape[1]
@@ -528,12 +546,12 @@
             stages[reached[piece]](piece)
             reached[piece] += 1
 
-    middle = rows // 2
+    middle = rows // 2 // GROUP
     for mode in range(mode_count):
-        lax.fori_loop(0, middle, back(mode), 0)
+        lax.fori_loop(0, middle, back(mode, GROUP), 0)
         for piece in range(mode):
             advance(piece)
-        lax.fori_loop(middle, rows, back(mode), 0)
+        lax.fori_loop(middle, 2 * middle, back(mode, GROUP), 0)
         for piece in range(mode - 1):
             advance(piece)
         pair_copy(mode).start()
@@ -544,15 +562,14 @@
         def _():
             object_halo(index).wait_send()
 
-    accumulate()
+    gradient[...] = jnp.zeros_like(gradient)
+    plan = ((1, 2), (0,), (1, 2), (0,))
+    for quarter, which in enumerate(plan):
+        accumulate(quarter * rows // 4, (quarter + 1) * rows // 4)
+        for piece in which:
+            advance(piece)
     for index, (down, across) in enumerate(DIRECTIONS):
-        if not down:
-            start_halo(index)
-    for piece in range(pieces):
-        advance(piece)
-    for index, (down, across) in enumerate(DIRECTIONS):
-        if down:
-            start_halo(index)
+        start_halo(index)
     folded[...] = gradient[:, half : half + tile, half : half + tile]
     for _ in stages:
         for piece in range(pieces):
@@ -628,7 +645,7 @@
             pltpu.VMEM((modes, points, 2 * points), f32),
             pltpu.VMEM((rows, 2, points, points), f32),
             pltpu.VMEM((modes, length, points), f32),
-            pltpu.VMEM((2 * tile + points, reach), f32),
+            pltpu.VMEM((2 * tile + points, 2 * tile + half), f32),
             pltpu.VMEM((2, 2, tile, half), f32),
             pltpu.VMEM((2, 2, half, tile), f32),
             pltpu.VMEM((4, 2, half, half), f32),

time: 112 us -> 101 us (0.902); the launches traced: 111 us -> 99.2 us
  Pallas kernels: 104 us -> 92.3 us
    pallas_call x1, Pallas kernels: 104 us -> 92.3 us  [whole(): pl.pallas_call(whole_kernel, name='whole', out_shape=(jax.ShapeDtypeStruc...]
where the time goes in v3:
time: 101 us; the launch traced here: 99.2 us
  Pallas kernels  92.3 us (91%)
  other arithmetic  3.5 us (3%)
  local copies, waits for them, and re-layouts  2.83 us (3%)
    pallas_call x1, Pallas kernels, whole(): pl.pallas_call(whole_kernel, name='whole', out_shape=(jax.ShapeDtypeStruc...  92.3 us
    mul x1, other arithmetic, shards(): summed.reshape(probe.shape) * (1.0 / math.sqrt(frame_total))  2.83 us
    unnamed x5, local copies, waits for them, and re-layouts  2.83 us

profile of v3, /device:TPU:0, one launch (start us, length us, event | category | flops | bytes accessed | tf_op | source)
XLA Modules:
  0.0 99.2 jit_solution(14821591696543382801)
XLA Ops:
  0.6 0.7 copy.10
  1.4 0.8 copy.11
  2.1 0.7 pad_add_fusion.table
  2.8 92.3 %whole.1 = (f32[2,512,512]{2,1,0:T(8,128)}, f32[3,512,256]{2,1,0:T(8,128)}) custom-call(s32[6,3]{1,0:T(8,128)} %pad_add_fusion.table, f32[2,512,512]{2,1,0:T(8,128)} %object_hbm.1, f32[3,2,256,256]{3,2,1,0:T(8,128)} %probe_hbm.1, bf16[6,256,256]{2,1,0:T(8,128)(2,1)} %raw_hbm.1, f32[256,256]{1,0:T(8,128)} %delta_hbm.1, ...), custom_call_target="tpu_custom_call" | custom-call | tf_op jit(solution)/shard_map/whole/pallas_call | solution.py:622
  95.1 0.0 copy-start
  95.1 2.8 %broadcast_multiply_fusion = f32[3,512,256]{2,1,0:T(8,128)} fusion(f32[3,512,256]{2,1,0:T(8,128)} %get-tuple-element.5), kind=kLoop, calls=%fused_computation | loop fusion | flops 393216 | bytes 3145728 | tf_op jit(solution)/shard_map/mul | solution.py:690
  97.9 0.0 copy-done
  97.9 1.3 %copy.13 = f32[2,512,512]{2,1,0:T(8,128)} copy(f32[2,512,512]{2,1,0:T(8,128)S(1)} %copy-done) | data formatting | bytes 4194304
Async XLA Ops:
  95.1 2.8 %copy-start = (f32[2,512,512]{2,1,0:T(8,128)S(1)}, f32[2,512,512]{2,1,0:T(8,128)}, u32[]{:S(2)}) copy-start(f32[2,512,512]{2,1,0:T(8,128)} %get-tuple-element.8) | copy-start | bytes 6291460

commit v4 on v3

--- a/solution.py
+++ b/solution.py
@@ -11,6 +11,7 @@
 
 MESH = pl.DeviceIdType.MESH
 GROUP = 2
+WAYS = 4
 DIRECTIONS = tuple(
     (down, across) for down in (-1, 0, 1) for across in (-1, 0, 1) if (down, across) != (0, 0)
 )
@@ -37,6 +38,24 @@
 def outer_edge(step, tile, half):
     start, size = {-1: (0, half), 0: (half, tile), 1: (half + tile, half)}[step]
     return pl.ds(start, size)
+
+
+LEVELS = 32767.0
+
+
+def coded(value, bound):
+    level = jnp.sqrt(jnp.abs(value) * (1.0 / bound)) * LEVELS
+    level = jnp.where(value < 0.0, -level, level)
+    return jnp.round(level).astype(jnp.int32).astype(jnp.int16)
+
+
+def decoded(code, bound):
+    level = code.astype(jnp.int32).astype(jnp.float32) * (1.0 / LEVELS)
+    return level * jnp.abs(level) * bound
+
+
+def greatest(value):
+    return jnp.maximum(jnp.max(jnp.abs(value)), 1e-30)
 
 
 def greet():
@@ -67,7 +86,8 @@
 
 
 def whole_kernel(
-    table,
+    tile_row,
+    offsets,
     object_hbm,
     probe_hbm,
     raw_hbm,
@@ -93,9 +113,14 @@
     terms,
     total,
     shifted,
+    code_tall,
+    code_wide,
+    code_corners,
     halos_tall,
     halos_wide,
     corners,
+    bound_out,
+    bounds,
     pair_in,
     pair_sum,
     chip_in,
@@ -113,6 +138,8 @@
     info_recv,
     halo_send,
     halo_recv,
+    bound_send,
+    bound_recv,
     pair_sems,
     chip_sems,
     line_sems,
@@ -151,10 +178,10 @@
     def chosen(other):
         pick, top, left, live = (jnp.int32(0), jnp.int32(0), jnp.int32(0), jnp.int32(0))
         for k in range(frame_count):
-            hit = table[k, 0] == other
+            hit = tile_row[k, 0] == other
             pick = jnp.where(hit, k, pick)
-            top = jnp.where(hit, table[k, 1], top)
-            left = jnp.where(hit, table[k, 2], left)
+            top = jnp.where(hit, offsets[k, 0], top)
+            left = jnp.where(hit, offsets[k, 1], left)
             live = jnp.where(hit, 1, live)
         return pick, top, left, live
 
@@ -195,6 +222,23 @@
         return carry
 
     lax.fori_loop(0, rows, tell, 0)
+
+    def pick(tall, wide, corner, index, part):
+        down, across = DIRECTIONS[index]
+        if down and across:
+            return corner.at[(down + 1) + (across + 1) // 2, part]
+        return wide.at[(down + 1) // 2, part] if down else tall.at[(across + 1) // 2, part]
+
+    def bound_copy(index):
+        down, across = DIRECTIONS[index]
+        return pltpu.make_async_remote_copy(
+            src_ref=bound_out,
+            dst_ref=bounds.at[index],
+            send_sem=bound_send.at[index],
+            recv_sem=bound_recv.at[index],
+            device_id=(row + down, col + across),
+            device_id_type=MESH,
+        )
 
     def object_halo(index):
         down, across = DIRECTIONS[index]
@@ -357,36 +401,36 @@
 
         return one
 
-    def accumulate(begin, end):
-        chunk = 64
-
-        def one(step, carry):
-            _, top, left, _ = spot(step)
-            skip_rows, skip_cols = (lax.rem(top, 8), lax.rem(left, 128))
-            base = tile // 8 - lax.div(top, 8)
-            across = (tile // 128 - 1 - lax.div(left, 128)) * 128
-            for part in range(2):
+    ways = shifted.shape[0]
+
+    def accumulate(group):
+        chunk = 32
+        first = group * ways
+        found = [spot(first + k) for k in range(ways)]
+        bases = [tile // 8 - lax.div(top, 8) for _, top, _, _ in found]
+        acrosses = [(tile // 128 - 1 - lax.div(left, 128)) * 128 for _, _, left, _ in found]
+        for part in range(2):
+            for k in range(ways):
+                _, top, left, _ = found[k]
                 block = jnp.concatenate(
-                    [terms[step, part], jnp.zeros((8, points), jnp.float32)], 0
+                    [terms[first + k, part], jnp.zeros((8, points), jnp.float32)], 0
                 )
-                block = pltpu.roll(block, skip_rows, 0)
+                block = pltpu.roll(block, lax.rem(top, 8), 0)
                 block = jnp.concatenate([block, jnp.zeros((span_rows, 128), jnp.float32)], 1)
-                shifted[pl.ds(tile, span_rows), pl.ds(tile - 128, span_cols)] = pltpu.roll(
-                    block, skip_cols, 1
+                shifted[k, pl.ds(tile, span_rows), pl.ds(tile - 128, span_cols)] = pltpu.roll(
+                    block, lax.rem(left, 128), 1
                 )
 
-                def add(index, inner):
-                    start = pl.multiple_of(index * chunk, 8)
-                    source = (base + index * (chunk // 8)) * 8
-                    gradient[part, pl.ds(start, chunk)] += shifted[
-                        pl.ds(source, chunk), pl.ds(across, reach)
-                    ]
-                    return inner
-
-                lax.fori_loop(0, reach // chunk, add, 0)
-            return carry
-
-        lax.fori_loop(begin, end, one, 0)
+            def add(index, inner):
+                start = pl.multiple_of(index * chunk, 8)
+                value = gradient[part, pl.ds(start, chunk)]
+                for k in range(ways):
+                    source = (bases[k] + index * (chunk // 8)) * 8
+                    value = value + shifted[k, pl.ds(source, chunk), pl.ds(acrosses[k], reach)]
+                gradient[part, pl.ds(start, chunk)] = value
+                return inner
+
+            lax.fori_loop(0, reach // chunk, add, 0)
 
     pieces = pair_in.shape[0]
     length = pair_in.shape[1]
@@ -403,29 +447,46 @@
         return pl.ds(pl.multiple_of((1 - core) * lanes, lanes), lanes)
 
     sibling = (row + 1 - 2 * core, col)
-    def landing(index):
-        down, across = DIRECTIONS[index]
-        if down and across:
-            return corners.at[(down + 1) + (across + 1) // 2]
-        return halos_wide.at[(down + 1) // 2] if down else halos_tall.at[(across + 1) // 2]
-
-    def halo(index):
+    def halo(index, part):
         down, across = DIRECTIONS[index]
         return pltpu.make_async_remote_copy(
-            src_ref=gradient.at[:, outer_edge(down, tile, half), outer_edge(across, tile, half)],
-            dst_ref=landing(index),
-            send_sem=halo_send.at[index],
-            recv_sem=halo_recv.at[index],
+            src_ref=pick(code_tall, code_wide, code_corners, index, part),
+            dst_ref=pick(halos_tall, halos_wide, corners, index, part),
+            send_sem=halo_send.at[part, index],
+            recv_sem=halo_recv.at[part, index],
             device_id=(row + down, col + across),
             device_id_type=MESH,
         )
 
-    def start_halo(index):
-        down, across = DIRECTIONS[index]
-
-        @pl.when(inside(row + down, col + across, rows, cols))
-        def _():
-            halo(index).start()
+    def encode(part, bound):
+        for index, (down, across) in enumerate(DIRECTIONS):
+            where = (part, outer_edge(down, tile, half), outer_edge(across, tile, half))
+            pick(code_tall, code_wide, code_corners, index, part)[...] = coded(
+                gradient[where], bound
+            )
+
+    def start_halos(part):
+        for index, (down, across) in enumerate(DIRECTIONS):
+
+            @pl.when(inside(row + down, col + across, rows, cols))
+            def _():
+                if part == 0:
+                    bound_copy(index).start()
+                halo(index, part).start()
+
+    def take_halos(part):
+        for index, (down, across) in enumerate(DIRECTIONS):
+
+            @pl.when(inside(row - down, col - across, rows, cols))
+            def _():
+                if part == 0:
+                    bound_copy(index).wait_recv()
+                halo(index, part).wait_recv()
+                where = (part, inner_edge(-down, tile, half), inner_edge(-across, tile, half))
+                folded[where] += decoded(
+                    pick(halos_tall, halos_wide, corners, index, part)[...],
+                    jnp.max(bounds[index]),
+                )
 
     def remote(source, target, sems, index, device):
         return pltpu.make_async_remote_copy(
@@ -563,33 +624,39 @@
             object_halo(index).wait_send()
 
     gradient[...] = jnp.zeros_like(gradient)
-    plan = ((1, 2), (0,), (1, 2), (0,))
-    for quarter, which in enumerate(plan):
-        accumulate(quarter * rows // 4, (quarter + 1) * rows // 4)
-        for piece in which:
+    passes = rows // ways
+    plan = (1, 2, 0, 1, 2, 0)
+    done = 0
+    for group in range(passes):
+        accumulate(group)
+        until = len(plan) * (group + 1) // passes
+        for piece in plan[done:until]:
             advance(piece)
-    for index, (down, across) in enumerate(DIRECTIONS):
-        start_halo(index)
+        done = until
+    bound = greatest(gradient[...])
+    bound_out[...] = jnp.full((8, 128), bound, jnp.float32)
+    encode(0, bound)
+    advance(1)
+    start_halos(0)
+    encode(1, bound)
+    advance(2)
     folded[...] = gradient[:, half : half + tile, half : half + tile]
+    advance(2)
+    start_halos(1)
     for _ in stages:
         for piece in range(pieces):
             advance(piece)
-
-    for index, (down, across) in enumerate(DIRECTIONS):
-
-        @pl.when(inside(row - down, col - across, rows, cols))
-        def _():
-            halo(index).wait_recv()
-            where = (slice(None), inner_edge(-down, tile, half), inner_edge(-across, tile, half))
-            folded[where] += landing(index)[...]
-
+    take_halos(0)
+    take_halos(1)
     for piece in range(pieces):
         back_pair_copy(piece).wait_recv()
     for index, (down, across) in enumerate(DIRECTIONS):
 
         @pl.when(inside(row + down, col + across, rows, cols))
         def _():
-            halo(index).wait_send()
+            bound_copy(index).wait_send()
+            halo(index, 0).wait_send()
+            halo(index, 1).wait_send()
 
     def sent(step, carry):
         slot_copy(step, row, lax.rem(row + step, rows)).wait_send()
@@ -607,7 +674,7 @@
             back_line_copy(piece, step).wait_send()
 
 
-def whole(table, object_field, probe, raw_counts, delta, forward, backward):
+def whole(tile_row, offsets, object_field, probe, raw_counts, delta, forward, backward):
     rows, cols = (lax.axis_size("row"), lax.axis_size("col"))
     tile = object_field.shape[1]
     modes, _, points, _ = probe.shape
@@ -615,7 +682,7 @@
     reach = tile + points
     length, lanes = (2 * points, points // 2)
     chips = rows // 2
-    f32, bf16, i32 = (jnp.float32, jnp.bfloat16, jnp.int32)
+    f32, bf16, i32, i16 = (jnp.float32, jnp.bfloat16, jnp.int32, jnp.int16)
     vmem = pl.BlockSpec(memory_space=pltpu.VMEM)
     hbm = pl.BlockSpec(memory_space=pl.ANY)
     dma = pltpu.SemaphoreType.DMA
@@ -626,7 +693,7 @@
             jax.ShapeDtypeStruct((2, tile, tile), f32),
             jax.ShapeDtypeStruct((modes, length, points), f32),
         ),
-        in_specs=[pl.BlockSpec(memory_space=pltpu.SMEM)] + [hbm] * 6,
+        in_specs=[pl.BlockSpec(memory_space=pltpu.SMEM)] * 2 + [hbm] * 6,
         out_specs=(vmem, vmem),
         scratch_shapes=[
             pltpu.VMEM(probe.shape, f32),
@@ -645,10 +712,15 @@
             pltpu.VMEM((modes, points, 2 * points), f32),
             pltpu.VMEM((rows, 2, points, points), f32),
             pltpu.VMEM((modes, length, points), f32),
-            pltpu.VMEM((2 * tile + points, 2 * tile + half), f32),
-            pltpu.VMEM((2, 2, tile, half), f32),
-            pltpu.VMEM((2, 2, half, tile), f32),
-            pltpu.VMEM((4, 2, half, half), f32),
+            pltpu.VMEM((WAYS if rows <= 8 else 1, 2 * tile + points, 2 * tile + half), f32),
+            pltpu.VMEM((2, 2, tile, half), i16),
+            pltpu.VMEM((2, 2, half, tile), i16),
+            pltpu.VMEM((4, 2, half, half), i16),
+            pltpu.VMEM((2, 2, tile, half), i16),
+            pltpu.VMEM((2, 2, half, tile), i16),
+            pltpu.VMEM((4, 2, half, half), i16),
+            pltpu.VMEM((8, 128), f32),
+            pltpu.VMEM((8, 8, 128), f32),
             pltpu.VMEM((modes, length, lanes), f32),
             pltpu.VMEM((modes, length, lanes), f32),
             pltpu.VMEM((modes * chips, length // chips, lanes), f32),
@@ -664,6 +736,8 @@
             dma((rows,)),
             dma((rows,)),
             dma((rows,)),
+            dma((2, 8)),
+            dma((2, 8)),
             dma((8,)),
             dma((8,)),
             dma((2, modes)),
@@ -676,16 +750,15 @@
         compiler_params=pltpu.CompilerParams(
             collective_id=0, has_side_effects=True, vmem_limit_bytes=67043328
         ),
-    )(table, object_field, probe, raw_counts, delta, forward, backward)
+    )(tile_row, offsets, object_field, probe, raw_counts, delta, forward, backward)
 
 
 def shards(object_field, probe, raw_counts, resample_delta, tile_row, offsets):
     points = probe.shape[-1]
     frame_total = raw_counts.shape[0] * lax.axis_size("row") * lax.axis_size("col")
     forward, backward = dft_tables(points)
-    table = jnp.concatenate([tile_row, offsets], 1)
     object_grad, summed = whole(
-        table, object_field, probe, raw_counts, resample_delta, forward, backward
+        tile_row, offsets, object_field, probe, raw_counts, resample_delta, forward, backward
     )
     return (object_grad, summed.reshape(probe.shape) * (1.0 / math.sqrt(frame_total)))
 

time: 101 us -> 91.5 us (0.906)
  Pallas kernels: 92.3 us -> 82.7 us
  local copies, waits for them, and re-layouts: 2.83 us -> 4 us
    pallas_call x1, Pallas kernels: 92.3 us -> 82.7 us  [whole(): pl.pallas_call(whole_kernel, name='whole', out_shape=(jax.ShapeDtypeStruc...]
    unnamed x5, local copies, waits for them, and re-layouts: 2.83 us -> 4 us
where the time goes in v4:
time: 91.5 us; the launch traced here: 90.2 us
  Pallas kernels  82.7 us (90%)
  local copies, waits for them, and re-layouts  4 us (4%)
  other arithmetic  2.83 us (3%)
    pallas_call x1, Pallas kernels, whole(): pl.pallas_call(whole_kernel, name='whole', out_shape=(jax.ShapeDtypeStruc...  82.7 us
    unnamed x5, local copies, waits for them, and re-layouts  4 us
    mul x1, other arithmetic, shards(): summed.reshape(probe.shape) * (1.0 / math.sqrt(frame_total))  2.83 us

profile of v4, /device:TPU:0, one launch (start us, length us, event | category | flops | bytes accessed | tf_op | source)
XLA Modules:
  0.0 90.2 jit_solution(9216229355745958735)
XLA Ops:
  0.6 1.3 %copy.10.tile_row = s32[6,1]{1,0:T(8,128)} copy(s32[6,1]{0,1:T(1,128)} %param.12) | data formatting | bytes 48 | tf_op args[4]
  2.0 1.4 %copy.11.offsets = s32[6,2]{1,0:T(8,128)} copy(s32[6,2]{0,1:T(2,128)} %param.13) | data formatting | bytes 96 | tf_op args[5]
  3.3 82.7 %whole.1 = (f32[2,512,512]{2,1,0:T(8,128)}, f32[3,512,256]{2,1,0:T(8,128)}) custom-call(s32[6,1]{1,0:T(8,128)} %copy.10.tile_row, s32[6,2]{1,0:T(8,128)} %copy.11.offsets, f32[2,512,512]{2,1,0:T(8,128)} %object_hbm.1, f32[3,2,256,256]{3,2,1,0:T(8,128)} %probe_hbm.1, bf16[6,256,256]{2,1,0:T(8,128)(2,1)} %raw_hbm.1, f32[256,256]{1,0:T(8,128)} %delta_hbm.1, ...), custom_call_target="tpu_custom_call" | custom-call | tf_op jit(solution)/shard_map/whole/pallas_call | solution.py:689
  86.1 0.0 copy-start
  86.1 2.8 %broadcast_multiply_fusion = f32[3,512,256]{2,1,0:T(8,128)} fusion(f32[3,512,256]{2,1,0:T(8,128)} %get-tuple-element.5), kind=kLoop, calls=%fused_computation | loop fusion | flops 393216 | bytes 3145728 | tf_op jit(solution)/shard_map/mul | solution.py:763
  88.9 0.0 copy-done
  88.9 1.3 %copy.13 = f32[2,512,512]{2,1,0:T(8,128)} copy(f32[2,512,512]{2,1,0:T(8,128)S(1)} %copy-done) | data formatting | bytes 4194304
Async XLA Ops:
  86.1 2.8 %copy-start = (f32[2,512,512]{2,1,0:T(8,128)S(1)}, f32[2,512,512]{2,1,0:T(8,128)}, u32[]{:S(2)}) copy-start(f32[2,512,512]{2,1,0:T(8,128)} %get-tuple-element.8) | copy-start | bytes 6291460

commit v5 on v4

--- a/solution.py
+++ b/solution.py
@@ -132,6 +132,7 @@
     local_sems,
     object_send,
     object_recv,
+    relay_sems,
     slot_send,
     slot_recv,
     info_send,
@@ -229,13 +230,13 @@
             return corner.at[(down + 1) + (across + 1) // 2, part]
         return wide.at[(down + 1) // 2, part] if down else tall.at[(across + 1) // 2, part]
 
-    def bound_copy(index):
+    def bound_copy(index, part):
         down, across = DIRECTIONS[index]
         return pltpu.make_async_remote_copy(
-            src_ref=bound_out,
-            dst_ref=bounds.at[index],
-            send_sem=bound_send.at[index],
-            recv_sem=bound_recv.at[index],
+            src_ref=bound_out.at[part],
+            dst_ref=bounds.at[part, index],
+            send_sem=bound_send.at[part, index],
+            recv_sem=bound_recv.at[part, index],
             device_id=(row + down, col + across),
             device_id_type=MESH,
         )
@@ -257,14 +258,57 @@
 
     for index, (down, across) in enumerate(DIRECTIONS):
 
-        @pl.when(inside(row + down, col + across, rows, cols))
-        def _():
-            object_halo(index).start()
+        if not (down and across):
+
+            @pl.when(inside(row + down, col + across, rows, cols))
+            def _():
+                object_halo(index).start()
 
         @pl.when(jnp.logical_not(inside(row - down, col - across, rows, cols)))
         def _():
             where = (slice(None), outer_edge(-down, tile, half), outer_edge(-across, tile, half))
             extended[where] = jnp.zeros((2, where[1].size, where[2].size), jnp.float32)
+
+    core = lax.rem(row, 2)
+    near = 1 - 2 * core
+    sides = ((0, -1), (1, 1))
+
+    def pair_relay(side, across):
+        source = pl.multiple_of(tile * (1 - core) + half * core, 8)
+        target = pl.multiple_of((half + tile) * core, 8)
+        lanes_at = outer_edge(across, tile, half)
+        return pltpu.make_async_remote_copy(
+            src_ref=extended.at[:, pl.ds(source, half), lanes_at],
+            dst_ref=extended.at[:, pl.ds(target, half), lanes_at],
+            send_sem=relay_sems.at[0, 0, side],
+            recv_sem=relay_sems.at[0, 1, side],
+            device_id=(row + near, col),
+            device_id_type=MESH,
+        )
+
+    def line_relay(side, across):
+        rows_at = pl.ds(pl.multiple_of((half + tile) * core, 8), half)
+        return pltpu.make_async_remote_copy(
+            src_ref=extended.at[:, rows_at, pl.ds(tile if across > 0 else half, half)],
+            dst_ref=extended.at[:, rows_at, outer_edge(-across, tile, half)],
+            send_sem=relay_sems.at[1, 0, side],
+            recv_sem=relay_sems.at[1, 1, side],
+            device_id=(row, col + across),
+            device_id_type=MESH,
+        )
+
+    def relayed(act_pair, act_line, sending):
+        for side, across in sides:
+
+            @pl.when(inside(row, col + across, rows, cols))
+            def _():
+                act_pair(pair_relay(side, across))
+
+            toward = across if sending else -across
+
+            @pl.when(inside(row - near, col + toward, rows, cols))
+            def _():
+                act_line(line_relay(side, across))
 
     loads[0].wait()
     loads[1].wait()
@@ -306,14 +350,36 @@
     noted.start()
     total[...] = jnp.zeros_like(total)
     shifted[...] = jnp.zeros_like(shifted)
+    for side, across in sides:
+
+        @pl.when(inside(row, col + across, rows, cols))
+        def _():
+            object_halo(DIRECTIONS.index((0, -across))).wait_recv()
+            pair_relay(side, across).start()
+
+    for which in range(2):
+        far = 2 * which - 1
+
+        @pl.when((core == which) & inside(row + far, col, rows, cols))
+        def _():
+            object_halo(DIRECTIONS.index((-far, 0))).wait_recv()
+
+    for side, across in sides:
+
+        @pl.when(inside(row - near, col + across, rows, cols))
+        def _():
+            line_relay(side, across).start()
+
+    for which in range(2):
+
+        @pl.when(core == which)
+        def _():
+            object_halo(DIRECTIONS.index((2 * which - 1, 0))).wait_recv()
+
     for load in loads[2:]:
         load.wait()
     noted.wait()
-    for index, (down, across) in enumerate(DIRECTIONS):
-
-        @pl.when(inside(row - down, col - across, rows, cols))
-        def _():
-            object_halo(index).wait_recv()
+    relayed(lambda copy: copy.wait_recv(), lambda copy: copy.wait_recv(), False)
 
     span_rows, span_cols = (points + 8, points + 128)
 
@@ -366,7 +432,7 @@
 
     lax.fori_loop(0, rows, onward, 0)
 
-    def back(mode, group):
+    def back(mode, group, middle, hook):
         def one(index, carry):
             steps = [index * group + k for k in range(group)]
             backs = [
@@ -397,45 +463,51 @@
                 sum_imag = sum_imag + (object_real * update_imag - object_imag * update_real)
             total[mode, :points] = sum_real
             total[mode, points:] = sum_imag
+            if hook:
+
+                @pl.when(index == middle)
+                def _():
+                    for piece in hook:
+                        advance(piece)
+
             return carry
 
         return one
 
     ways = shifted.shape[0]
 
-    def accumulate(group):
+    def accumulate(part, group):
         chunk = 32
         first = group * ways
         found = [spot(first + k) for k in range(ways)]
         bases = [tile // 8 - lax.div(top, 8) for _, top, _, _ in found]
         acrosses = [(tile // 128 - 1 - lax.div(left, 128)) * 128 for _, _, left, _ in found]
-        for part in range(2):
+        for k in range(ways):
+            _, top, left, _ = found[k]
+            block = jnp.concatenate(
+                [terms[first + k, part], jnp.zeros((8, points), jnp.float32)], 0
+            )
+            block = pltpu.roll(block, lax.rem(top, 8), 0)
+            block = jnp.concatenate([block, jnp.zeros((span_rows, 128), jnp.float32)], 1)
+            shifted[k, pl.ds(tile, span_rows), pl.ds(tile - 128, span_cols)] = pltpu.roll(
+                block, lax.rem(left, 128), 1
+            )
+
+        def add(index, inner):
+            start = pl.multiple_of(index * chunk, 8)
+            value = gradient[part, pl.ds(start, chunk)]
             for k in range(ways):
-                _, top, left, _ = found[k]
-                block = jnp.concatenate(
-                    [terms[first + k, part], jnp.zeros((8, points), jnp.float32)], 0
-                )
-                block = pltpu.roll(block, lax.rem(top, 8), 0)
-                block = jnp.concatenate([block, jnp.zeros((span_rows, 128), jnp.float32)], 1)
-                shifted[k, pl.ds(tile, span_rows), pl.ds(tile - 128, span_cols)] = pltpu.roll(
-                    block, lax.rem(left, 128), 1
-                )
-
-            def add(index, inner):
-                start = pl.multiple_of(index * chunk, 8)
-                value = gradient[part, pl.ds(start, chunk)]
-                for k in range(ways):
-                    source = (bases[k] + index * (chunk // 8)) * 8
-                    value = value + shifted[k, pl.ds(source, chunk), pl.ds(acrosses[k], reach)]
-                gradient[part, pl.ds(start, chunk)] = value
-                return inner
-
-            lax.fori_loop(0, reach // chunk, add, 0)
+                source = (bases[k] + index * (chunk // 8)) * 8
+                value = value + shifted[k, pl.ds(source, chunk), pl.ds(acrosses[k], reach)]
+            gradient[part, pl.ds(start, chunk)] = value
+            return inner
+
+        lax.fori_loop(0, reach // chunk, add, 0)
 
     pieces = pair_in.shape[0]
     length = pair_in.shape[1]
     chips = rows // 2
-    core, chip = (lax.rem(row, 2), row // 2)
+    chip = row // 2
     chip_rows = length // chips
     line_rows = chip_rows // cols
     lanes = summed.shape[2] // 2
@@ -470,8 +542,7 @@
 
             @pl.when(inside(row + down, col + across, rows, cols))
             def _():
-                if part == 0:
-                    bound_copy(index).start()
+                bound_copy(index, part).start()
                 halo(index, part).start()
 
     def take_halos(part):
@@ -479,13 +550,12 @@
 
             @pl.when(inside(row - down, col - across, rows, cols))
             def _():
-                if part == 0:
-                    bound_copy(index).wait_recv()
+                bound_copy(index, part).wait_recv()
                 halo(index, part).wait_recv()
                 where = (part, inner_edge(-down, tile, half), inner_edge(-across, tile, half))
                 folded[where] += decoded(
                     pick(halos_tall, halos_wide, corners, index, part)[...],
-                    jnp.max(bounds[index]),
+                    jnp.max(bounds[part, index]),
                 )
 
     def remote(source, target, sems, index, device):
@@ -607,46 +677,45 @@
             stages[reached[piece]](piece)
             reached[piece] += 1
 
-    middle = rows // 2 // GROUP
+    middle = rows // 2 // GROUP - 1
     for mode in range(mode_count):
-        lax.fori_loop(0, middle, back(mode, GROUP), 0)
-        for piece in range(mode):
-            advance(piece)
-        lax.fori_loop(middle, 2 * middle, back(mode, GROUP), 0)
-        for piece in range(mode - 1):
-            advance(piece)
+        hook = tuple(range(mode))
+        lax.fori_loop(0, rows // GROUP, back(mode, GROUP, middle, hook), 0)
         pair_copy(mode).start()
 
     for index, (down, across) in enumerate(DIRECTIONS):
 
-        @pl.when(inside(row + down, col + across, rows, cols))
-        def _():
-            object_halo(index).wait_send()
+        if not (down and across):
+
+            @pl.when(inside(row + down, col + across, rows, cols))
+            def _():
+                object_halo(index).wait_send()
+
+    relayed(lambda copy: copy.wait_send(), lambda copy: copy.wait_send(), True)
 
     gradient[...] = jnp.zeros_like(gradient)
     passes = rows // ways
-    plan = (1, 2, 0, 1, 2, 0)
-    done = 0
-    for group in range(passes):
-        accumulate(group)
-        until = len(plan) * (group + 1) // passes
-        for piece in plan[done:until]:
-            advance(piece)
-        done = until
-    bound = greatest(gradient[...])
-    bound_out[...] = jnp.full((8, 128), bound, jnp.float32)
-    encode(0, bound)
+    for part, which in enumerate(((0, 1, 2), (0, 1, 2))):
+        for group in range(passes):
+            accumulate(part, group)
+            if group == (passes - 1) // 2:
+                for piece in which:
+                    advance(piece)
+        bound = greatest(gradient[part])
+        bound_out[part] = jnp.full((8, 128), bound, jnp.float32)
+        encode(part, bound)
+        if part == 0:
+            start_halos(0)
     advance(1)
-    start_halos(0)
-    encode(1, bound)
     advance(2)
+    start_halos(1)
+    advance(0)
     folded[...] = gradient[:, half : half + tile, half : half + tile]
     advance(2)
-    start_halos(1)
+    take_halos(0)
     for _ in stages:
         for piece in range(pieces):
             advance(piece)
-    take_halos(0)
     take_halos(1)
     for piece in range(pieces):
         back_pair_copy(piece).wait_recv()
@@ -654,7 +723,8 @@
 
         @pl.when(inside(row + down, col + across, rows, cols))
         def _():
-            bound_copy(index).wait_send()
+            bound_copy(index, 0).wait_send()
+            bound_copy(index, 1).wait_send()
             halo(index, 0).wait_send()
             halo(index, 1).wait_send()
 
@@ -719,8 +789,8 @@
             pltpu.VMEM((2, 2, tile, half), i16),
             pltpu.VMEM((2, 2, half, tile), i16),
             pltpu.VMEM((4, 2, half, half), i16),
-            pltpu.VMEM((8, 128), f32),
-            pltpu.VMEM((8, 8, 128), f32),
+            pltpu.VMEM((2, 8, 128), f32),
+            pltpu.VMEM((2, 8, 8, 128), f32),
             pltpu.VMEM((modes, length, lanes), f32),
             pltpu.VMEM((modes, length, lanes), f32),
             pltpu.VMEM((modes * chips, length // chips, lanes), f32),
@@ -732,14 +802,15 @@
             dma((7,)),
             dma((8,)),
             dma((8,)),
+            dma((2, 2, 2)),
             dma((rows,)),
             dma((rows,)),
             dma((rows,)),
             dma((rows,)),
             dma((2, 8)),
             dma((2, 8)),
-            dma((8,)),
-            dma((8,)),
+            dma((2, 8)),
+            dma((2, 8)),
             dma((2, modes)),
             dma((2, modes * chips)),
             dma((2, modes * cols)),

time: 91.5 us -> 87.3 us (0.954); the launches traced: 90.2 us -> 87 us
  Pallas kernels: 82.7 us -> 79.6 us
    pallas_call x1, Pallas kernels: 82.7 us -> 79.6 us  [whole(): pl.pallas_call(whole_kernel, name='whole', out_shape=(jax.ShapeDtypeStruc...]
where the time goes in v5:
time: 87.3 us; the launch traced here: 87 us
  Pallas kernels  79.6 us (91%)
  local copies, waits for them, and re-layouts  4 us (5%)
  other arithmetic  2.83 us (3%)
    pallas_call x1, Pallas kernels, whole(): pl.pallas_call(whole_kernel, name='whole', out_shape=(jax.ShapeDtypeStruc...  79.6 us
    unnamed x5, local copies, waits for them, and re-layouts  4 us
    mul x1, other arithmetic, shards(): summed.reshape(probe.shape) * (1.0 / math.sqrt(frame_total))  2.83 us

profile of v5, /device:TPU:0, one launch (start us, length us, event | category | flops | bytes accessed | tf_op | source)
XLA Modules:
  0.0 87.0 jit_solution(16670440722925731933)
XLA Ops:
  0.6 1.3 %copy.10.tile_row = s32[6,1]{1,0:T(8,128)} copy(s32[6,1]{0,1:T(1,128)} %param.12) | data formatting | bytes 48 | tf_op args[4]
  2.0 1.4 %copy.11.offsets = s32[6,2]{1,0:T(8,128)} copy(s32[6,2]{0,1:T(2,128)} %param.13) | data formatting | bytes 96 | tf_op args[5]
  3.3 79.6 %whole.1 = (f32[2,512,512]{2,1,0:T(8,128)}, f32[3,512,256]{2,1,0:T(8,128)}) custom-call(s32[6,1]{1,0:T(8,128)} %copy.10.tile_row, s32[6,2]{1,0:T(8,128)} %copy.11.offsets, f32[2,512,512]{2,1,0:T(8,128)} %object_hbm.1, f32[3,2,256,256]{3,2,1,0:T(8,128)} %probe_hbm.1, bf16[6,256,256]{2,1,0:T(8,128)(2,1)} %raw_hbm.1, f32[256,256]{1,0:T(8,128)} %delta_hbm.1, ...), custom_call_target="tpu_custom_call" | custom-call | tf_op jit(solution)/shard_map/whole/pallas_call | solution.py:759
  82.9 0.0 copy-start
  82.9 2.8 %broadcast_multiply_fusion = f32[3,512,256]{2,1,0:T(8,128)} fusion(f32[3,512,256]{2,1,0:T(8,128)} %get-tuple-element.5), kind=kLoop, calls=%fused_computation | loop fusion | flops 393216 | bytes 3145728 | tf_op jit(solution)/shard_map/mul | solution.py:834
  85.7 0.0 copy-done
  85.7 1.3 %copy.13 = f32[2,512,512]{2,1,0:T(8,128)} copy(f32[2,512,512]{2,1,0:T(8,128)S(1)} %copy-done) | data formatting | bytes 4194304
Async XLA Ops:
  82.9 2.8 %copy-start = (f32[2,512,512]{2,1,0:T(8,128)S(1)}, f32[2,512,512]{2,1,0:T(8,128)}, u32[]{:S(2)}) copy-start(f32[2,512,512]{2,1,0:T(8,128)} %get-tuple-element.8) | copy-start | bytes 6291460

commit v6 on v5

--- a/solution.py
+++ b/solution.py
@@ -94,8 +94,11 @@
     delta_hbm,
     forward_hbm,
     backward_hbm,
+    folded_out,
+    summed_out,
     folded,
     summed,
+    out_sems,
     probe,
     raw,
     delta,
@@ -179,10 +182,10 @@
     def chosen(other):
         pick, top, left, live = (jnp.int32(0), jnp.int32(0), jnp.int32(0), jnp.int32(0))
         for k in range(frame_count):
-            hit = tile_row[k, 0] == other
+            hit = tile_row[0, k] == other
             pick = jnp.where(hit, k, pick)
-            top = jnp.where(hit, offsets[k, 0], top)
-            left = jnp.where(hit, offsets[k, 1], left)
+            top = jnp.where(hit, offsets[0, k], top)
+            left = jnp.where(hit, offsets[1, k], left)
             live = jnp.where(hit, 1, live)
         return pick, top, left, live
 
@@ -243,26 +246,40 @@
 
     def object_halo(index):
         down, across = DIRECTIONS[index]
+        if down:
+            start, size = {-1: (0, half), 0: (half, tile - points), 1: (tile - half, half)}[across]
+            lanes_from, lanes_to = (pl.ds(start, size), pl.ds(half + start, size))
+            device = (row + down, col)
+        else:
+            lanes_from = inner_edge(across, tile, half)
+            lanes_to = outer_edge(-across, tile, half)
+            device = (row, col + across)
         return pltpu.make_async_remote_copy(
-            src_ref=object_hbm.at[
-                :, inner_edge(down, tile, half), inner_edge(across, tile, half)
-            ],
-            dst_ref=extended.at[
-                :, outer_edge(-down, tile, half), outer_edge(-across, tile, half)
-            ],
+            src_ref=object_hbm.at[:, inner_edge(down, tile, half), lanes_from],
+            dst_ref=extended.at[:, outer_edge(-down, tile, half), lanes_to],
             send_sem=object_send.at[index],
             recv_sem=object_recv.at[index],
-            device_id=(row + down, col + across),
+            device_id=device,
             device_id_type=MESH,
         )
 
+    def strips(down):
+        return [DIRECTIONS.index((down, across)) for across in (-1, 1, 0)]
+
+    for down in (-1, 1):
+
+        @pl.when(inside(row + down, col, rows, cols))
+        def _():
+            for index in strips(down):
+                object_halo(index).start()
+
+    for across in (-1, 1):
+
+        @pl.when(inside(row, col + across, rows, cols))
+        def _():
+            object_halo(DIRECTIONS.index((0, across))).start()
+
     for index, (down, across) in enumerate(DIRECTIONS):
-
-        if not (down and across):
-
-            @pl.when(inside(row + down, col + across, rows, cols))
-            def _():
-                object_halo(index).start()
 
         @pl.when(jnp.logical_not(inside(row - down, col - across, rows, cols)))
         def _():
@@ -350,6 +367,20 @@
     noted.start()
     total[...] = jnp.zeros_like(total)
     shifted[...] = jnp.zeros_like(shifted)
+    for which in range(2):
+        far = 2 * which - 1
+
+        @pl.when((core == which) & inside(row + far, col, rows, cols))
+        def _():
+            for index in strips(-far)[:2]:
+                object_halo(index).wait_recv()
+
+    for side, across in sides:
+
+        @pl.when(inside(row - near, col + across, rows, cols))
+        def _():
+            line_relay(side, across).start()
+
     for side, across in sides:
 
         @pl.when(inside(row, col + across, rows, cols))
@@ -362,19 +393,12 @@
 
         @pl.when((core == which) & inside(row + far, col, rows, cols))
         def _():
-            object_halo(DIRECTIONS.index((-far, 0))).wait_recv()
-
-    for side, across in sides:
-
-        @pl.when(inside(row - near, col + across, rows, cols))
-        def _():
-            line_relay(side, across).start()
-
-    for which in range(2):
+            object_halo(strips(-far)[2]).wait_recv()
 
         @pl.when(core == which)
         def _():
-            object_halo(DIRECTIONS.index((2 * which - 1, 0))).wait_recv()
+            for index in strips(far):
+                object_halo(index).wait_recv()
 
     for load in loads[2:]:
         load.wait()
@@ -387,50 +411,63 @@
         source = lax.rem(row - step + rows, rows)
         return source, places[source, 0, 0], places[source, 0, 1], places[source, 0, 2]
 
-    def onward(step, carry):
-        source, top, left, live = spot(step)
-        skip_rows, skip_cols = (lax.rem(top, 8), lax.rem(left, 128))
-        across_rows = pl.ds(lax.div(top, 8) * 8, span_rows)
-        across_cols = pl.ds(lax.div(left, 128) * 128, span_cols)
-        for part in range(2):
-            block = extended[part, across_rows, across_cols]
-            block = pltpu.roll(block, lax.rem(span_cols - skip_cols, span_cols), 1)
-            block = block[:, :points]
-            block = pltpu.roll(block, lax.rem(span_rows - skip_rows, span_rows), 0)
-            windows[step, part] = block[:points]
-        intensity = jnp.zeros((points, points), jnp.float32)
+    def onward(pair, carry):
+        steps = [pair * GROUP + k for k in range(GROUP)]
+        spots = [spot(step) for step in steps]
+        for step, (_, top, left, _) in zip(steps, spots):
+            skip_rows, skip_cols = (lax.rem(top, 8), lax.rem(left, 128))
+            across_rows = pl.ds(lax.div(top, 8) * 8, span_rows)
+            across_cols = pl.ds(lax.div(left, 128) * 128, span_cols)
+            for part in range(2):
+                block = extended[part, across_rows, across_cols]
+                block = pltpu.roll(block, lax.rem(span_cols - skip_cols, span_cols), 1)
+                block = block[:, :points]
+                block = pltpu.roll(block, lax.rem(span_rows - skip_rows, span_rows), 0)
+                windows[step, part] = block[:points]
         halves = []
-        for mode in range(mode_count):
-            object_real, object_imag = (windows[step, 0], windows[step, 1])
-            probe_real, probe_imag = (probe[mode, 0], probe[mode, 1])
-            wave = jnp.concatenate(
-                [
-                    (probe_real * object_real - probe_imag * object_imag).astype(jnp.bfloat16),
-                    (probe_real * object_imag + probe_imag * object_real).astype(jnp.bfloat16),
-                ],
-                0,
-            )
-            halves.append(product(forward[...], wave).astype(jnp.bfloat16))
-        for mode, half_done in enumerate(halves):
-            wave_rows = jnp.concatenate([half_done[:points], half_done[points:]], 1)
-            field = product(wave_rows, backward[...])
-            far_field[mode] = field
-            squares = field * field
-            intensity = intensity + squares[:, :points] + squares[:, points:]
-
-        @pl.when(step > 0)
-        def _():
-            slot_copy(step, source, source).wait_recv()
-
-        amplitude = incoming[source].astype(jnp.float32)
-        scaling = 1.0 - amplitude / jnp.sqrt(jnp.maximum(intensity, 1.0))
-        scaling = scaling * live.astype(jnp.float32)
-        scaling = jnp.concatenate([scaling, scaling], 1)
-        for mode in range(mode_count):
-            residuals[step, mode] = (far_field[mode] * scaling).astype(jnp.bfloat16)
+        for step in steps:
+            for mode in range(mode_count):
+                object_real, object_imag = (windows[step, 0], windows[step, 1])
+                probe_real, probe_imag = (probe[mode, 0], probe[mode, 1])
+                wave = jnp.concatenate(
+                    [
+                        (probe_real * object_real - probe_imag * object_imag).astype(
+                            jnp.bfloat16
+                        ),
+                        (probe_real * object_imag + probe_imag * object_real).astype(
+                            jnp.bfloat16
+                        ),
+                    ],
+                    0,
+                )
+                halves.append(product(forward[...], wave).astype(jnp.bfloat16))
+        intensities = []
+        for k in range(GROUP):
+            intensity = jnp.zeros((points, points), jnp.float32)
+            for mode in range(mode_count):
+                half_done = halves[k * mode_count + mode]
+                wave_rows = jnp.concatenate([half_done[:points], half_done[points:]], 1)
+                field = product(wave_rows, backward[...])
+                far_field[k, mode] = field
+                squares = field * field
+                intensity = intensity + squares[:, :points] + squares[:, points:]
+            intensities.append(intensity)
+        for step, (source, _, _, _) in zip(steps, spots):
+
+            @pl.when(step > 0)
+            def _():
+                slot_copy(step, source, source).wait_recv()
+
+        for k, (step, (source, _, _, live)) in enumerate(zip(steps, spots)):
+            amplitude = incoming[source].astype(jnp.float32)
+            scaling = 1.0 - amplitude / jnp.sqrt(jnp.maximum(intensities[k], 1.0))
+            scaling = scaling * live.astype(jnp.float32)
+            scaling = jnp.concatenate([scaling, scaling], 1)
+            for mode in range(mode_count):
+                residuals[step, mode] = (far_field[k, mode] * scaling).astype(jnp.bfloat16)
         return carry
 
-    lax.fori_loop(0, rows, onward, 0)
+    lax.fori_loop(0, rows // GROUP, onward, 0)
 
     def back(mode, group, middle, hook):
         def one(index, carry):
@@ -508,6 +545,16 @@
     length = pair_in.shape[1]
     chips = rows // 2
     chip = row // 2
+    norming = 1.0 / math.sqrt(frame_count * rows * cols)
+
+    def folded_copy(part):
+        return pltpu.make_async_copy(folded.at[part], folded_out.at[part], out_sems.at[0, part])
+
+    def summed_copy(piece):
+        return pltpu.make_async_copy(
+            summed.at[piece], summed_out.at[piece], out_sems.at[1, piece]
+        )
+
     chip_rows = length // chips
     line_rows = chip_rows // cols
     lanes = summed.shape[2] // 2
@@ -537,8 +584,10 @@
                 gradient[where], bound
             )
 
-    def start_halos(part):
+    def start_halos(part, wanted=(-1, 0, 1)):
         for index, (down, across) in enumerate(DIRECTIONS):
+            if down not in wanted:
+                continue
 
             @pl.when(inside(row + down, col + across, rows, cols))
             def _():
@@ -650,6 +699,7 @@
         for step in range(1, cols):
             line_copy(piece, step).wait_recv()
             value = value + line_in[piece * cols + step]
+        value = value * norming
         line_sum[piece] = value
         line_out[piece, pl.ds(start, line_rows)] = value
         for step in range(1, cols):
@@ -679,17 +729,16 @@
 
     middle = rows // 2 // GROUP - 1
     for mode in range(mode_count):
-        hook = tuple(range(mode))
+        hook = (mode - 1,) if mode else ()
         lax.fori_loop(0, rows // GROUP, back(mode, GROUP, middle, hook), 0)
         pair_copy(mode).start()
+    advance(0)
 
     for index, (down, across) in enumerate(DIRECTIONS):
 
-        if not (down and across):
-
-            @pl.when(inside(row + down, col + across, rows, cols))
-            def _():
-                object_halo(index).wait_send()
+        @pl.when(inside(row + down, col + (0 if down else across), rows, cols))
+        def _():
+            object_halo(index).wait_send()
 
     relayed(lambda copy: copy.wait_send(), lambda copy: copy.wait_send(), True)
 
@@ -708,17 +757,21 @@
             start_halos(0)
     advance(1)
     advance(2)
-    start_halos(1)
+    start_halos(1, (0,))
     advance(0)
     folded[...] = gradient[:, half : half + tile, half : half + tile]
     advance(2)
+    start_halos(1, (-1, 1))
     take_halos(0)
+    folded_copy(0).start()
     for _ in stages:
         for piece in range(pieces):
             advance(piece)
     take_halos(1)
+    folded_copy(1).start()
     for piece in range(pieces):
         back_pair_copy(piece).wait_recv()
+        summed_copy(piece).start()
     for index, (down, across) in enumerate(DIRECTIONS):
 
         @pl.when(inside(row + down, col + across, rows, cols))
@@ -742,6 +795,10 @@
         for step in range(1, cols):
             line_copy(piece, step).wait_send()
             back_line_copy(piece, step).wait_send()
+    for part in range(2):
+        folded_copy(part).wait()
+    for piece in range(pieces):
+        summed_copy(piece).wait()
 
 
 def whole(tile_row, offsets, object_field, probe, raw_counts, delta, forward, backward):
@@ -764,8 +821,11 @@
             jax.ShapeDtypeStruct((modes, length, points), f32),
         ),
         in_specs=[pl.BlockSpec(memory_space=pltpu.SMEM)] * 2 + [hbm] * 6,
-        out_specs=(vmem, vmem),
+        out_specs=(hbm, hbm),
         scratch_shapes=[
+            pltpu.VMEM((2, tile, tile), f32),
+            pltpu.VMEM((modes, length, points), f32),
+            dma((2, max(2, modes))),
             pltpu.VMEM(probe.shape, f32),
             pltpu.VMEM(raw_counts.shape, bf16),
             pltpu.VMEM(delta.shape, f32),
@@ -779,7 +839,7 @@
             pltpu.SMEM((rows, 8, 128), i32),
             pltpu.VMEM((rows, 2, points, points), f32),
             pltpu.VMEM((rows, modes, points, 2 * points), bf16),
-            pltpu.VMEM((modes, points, 2 * points), f32),
+            pltpu.VMEM((GROUP, modes, points, 2 * points), f32),
             pltpu.VMEM((rows, 2, points, points), f32),
             pltpu.VMEM((modes, length, points), f32),
             pltpu.VMEM((WAYS if rows <= 8 else 1, 2 * tile + points, 2 * tile + half), f32),
@@ -826,12 +886,11 @@
 
 def shards(object_field, probe, raw_counts, resample_delta, tile_row, offsets):
     points = probe.shape[-1]
-    frame_total = raw_counts.shape[0] * lax.axis_size("row") * lax.axis_size("col")
     forward, backward = dft_tables(points)
     object_grad, summed = whole(
-        tile_row, offsets, object_field, probe, raw_counts, resample_delta, forward, backward
+        tile_row.T, offsets.T, object_field, probe, raw_counts, resample_delta, forward, backward
     )
-    return (object_grad, summed.reshape(probe.shape) * (1.0 / math.sqrt(frame_total)))
+    return (object_grad, summed.reshape(probe.shape))
 
 
 def solution(mesh):

time: 87.3 us -> 81.7 us (0.936)
  Pallas kernels: 79.6 us -> 75.6 us
  other arithmetic: 2.83 us -> 0 us
    pallas_call x1, Pallas kernels: 79.6 us -> 75.6 us  [whole(): pl.pallas_call(whole_kernel, name='whole', out_shape=(jax.ShapeDtypeStruc...]
    mul x1 -> x0, other arithmetic: 2.83 us -> none  [shards(): summed.reshape(probe.shape) * (1.0 / math.sqrt(frame_total))]
    unnamed x5 -> x4, local copies, waits for them, and re-layouts: 4 us -> 4.34 us
where the time goes in v6:
time: 81.7 us; the launch traced here: 80.6 us
  Pallas kernels  75.6 us (93%)
  local copies, waits for them, and re-layouts  4.34 us (5%)
    pallas_call x1, Pallas kernels, whole(): pl.pallas_call(whole_kernel, name='whole', out_shape=(jax.ShapeDtypeStruc...  75.6 us
    unnamed x4, local copies, waits for them, and re-layouts  4.34 us

profile of v6, /device:TPU:0, one launch (start us, length us, event | category | flops | bytes accessed | tf_op | source)
XLA Modules:
  0.0 80.6 jit_solution(13171700778787732654)
XLA Ops:
  0.6 75.6 %whole.1 = (f32[2,512,512]{2,1,0:T(8,128)}, f32[3,512,256]{2,1,0:T(8,128)}) custom-call(s32[1,6]{1,0:T(1,128)} %bitcast.5, s32[2,6]{1,0:T(2,128)} %bitcast.4, f32[2,512,512]{2,1,0:T(8,128)} %object_hbm.1, f32[3,2,256,256]{3,2,1,0:T(8,128)} %probe_hbm.1, bf16[6,256,256]{2,1,0:T(8,128)(2,1)} %raw_hbm.1, f32[256,256]{1,0:T(8,128)} %delta_hbm.1, ...), custom_call_target="tpu_custom_call" | custom-call | tf_op jit(solution)/shard_map/whole/pallas_call | solution.py:816
  76.3 0.0 copy-start
  76.3 3.2 %copy.12 = f32[2,512,512]{2,1,0:T(8,128)} copy(f32[2,512,512]{2,1,0:T(8,128)} %get-tuple-element.8) | data formatting | bytes 4194304
  79.5 0.0 copy-done
  79.5 1.1 %copy.13 = f32[3,2,256,256]{3,2,1,0:T(8,128)} copy(f32[3,2,256,256]{3,2,1,0:T(8,128)S(1)} %bitcast.3) | data formatting | bytes 3145728
Async XLA Ops:
  76.3 3.2 %copy-start = (f32[3,512,256]{2,1,0:T(8,128)S(1)}, f32[3,512,256]{2,1,0:T(8,128)}, u32[]{:S(2)}) copy-start(f32[3,512,256]{2,1,0:T(8,128)} %get-tuple-element.5) | copy-start | bytes 4718596

commit v7 on v6

--- a/solution.py
+++ b/solution.py
@@ -11,6 +11,7 @@
 
 MESH = pl.DeviceIdType.MESH
 GROUP = 2
+BACK_GROUP = 4
 WAYS = 4
 DIRECTIONS = tuple(
     (down, across) for down in (-1, 0, 1) for across in (-1, 0, 1) if (down, across) != (0, 0)
@@ -727,10 +728,10 @@
             stages[reached[piece]](piece)
             reached[piece] += 1
 
-    middle = rows // 2 // GROUP - 1
+    middle = rows // 2 // BACK_GROUP - 1
     for mode in range(mode_count):
         hook = (mode - 1,) if mode else ()
-        lax.fori_loop(0, rows // GROUP, back(mode, GROUP, middle, hook), 0)
+        lax.fori_loop(0, rows // BACK_GROUP, back(mode, BACK_GROUP, middle, hook), 0)
         pair_copy(mode).start()
     advance(0)
 
@@ -884,12 +885,49 @@
     )(tile_row, offsets, object_field, probe, raw_counts, delta, forward, backward)
 
 
+def finish_kernel(folded_in, summed_in, folded_out, summed_out, folded, summed, sems):
+    moves = [(folded_in, folded, folded_out, part) for part in range(folded.shape[0])]
+    moves += [(summed_in, summed, summed_out, piece) for piece in range(summed.shape[0])]
+    loads = []
+    stores = []
+    for i, (source, held, target, k) in enumerate(moves):
+        loads.append(pltpu.make_async_copy(source.at[k], held.at[k], sems.at[0, i]))
+        stores.append(pltpu.make_async_copy(held.at[k], target.at[k], sems.at[1, i]))
+    for load in loads:
+        load.start()
+    for load, store in zip(loads, stores):
+        load.wait()
+        store.start()
+    for store in stores:
+        store.wait()
+
+
+def finish(folded, summed):
+    hbm = pl.BlockSpec(memory_space=pl.ANY)
+    return pl.pallas_call(
+        finish_kernel,
+        name="finish",
+        out_shape=(
+            jax.ShapeDtypeStruct(folded.shape, folded.dtype),
+            jax.ShapeDtypeStruct(summed.shape, summed.dtype),
+        ),
+        in_specs=[hbm, hbm],
+        out_specs=(hbm, hbm),
+        scratch_shapes=[
+            pltpu.VMEM(folded.shape, folded.dtype),
+            pltpu.VMEM(summed.shape, summed.dtype),
+            pltpu.SemaphoreType.DMA((2, folded.shape[0] + summed.shape[0])),
+        ],
+    )(folded, summed)
+
+
 def shards(object_field, probe, raw_counts, resample_delta, tile_row, offsets):
     points = probe.shape[-1]
     forward, backward = dft_tables(points)
     object_grad, summed = whole(
         tile_row.T, offsets.T, object_field, probe, raw_counts, resample_delta, forward, backward
     )
+    object_grad, summed = finish(object_grad, summed)
     return (object_grad, summed.reshape(probe.shape))
 
 

time: 81.7 us -> 79.6 us (0.974)
  local copies, waits for them, and re-layouts: 4.34 us -> 0 us
  Pallas kernels: 75.6 us -> 77.6 us
    unnamed x4 -> x0, local copies, waits for them, and re-layouts: 4.34 us -> none
    pallas_call x0 -> x1, Pallas kernels: none -> 3.14 us  [finish(): pl.pallas_call(finish_kernel, name='finish', out_shape=(jax.ShapeDtypeStr...]
    pallas_call x1, Pallas kernels: 75.6 us -> 74.4 us  [whole(): pl.pallas_call(whole_kernel, name='whole', out_shape=(jax.ShapeDtypeStruc...]
where the time goes in v7:
time: 79.6 us; the launch traced here: 78.4 us
  Pallas kernels  77.6 us (97%)
  between operations  0.8 us (1%)
    pallas_call x1, Pallas kernels, whole(): pl.pallas_call(whole_kernel, name='whole', out_shape=(jax.ShapeDtypeStruc...  74.4 us
    pallas_call x1, Pallas kernels, finish(): pl.pallas_call(finish_kernel, name='finish', out_shape=(jax.ShapeDtypeStr...  3.14 us

profile of v7, /device:TPU:0, one launch (start us, length us, event | category | flops | bytes accessed | tf_op | source)
XLA Modules:
  0.0 78.4 jit_solution(17080215001953040496)
XLA Ops:
  0.6 74.4 %whole.1 = (f32[2,512,512]{2,1,0:T(8,128)}, f32[3,512,256]{2,1,0:T(8,128)}) custom-call(s32[1,6]{1,0:T(1,128)} %bitcast.4, s32[2,6]{1,0:T(2,128)} %bitcast.3, f32[2,512,512]{2,1,0:T(8,128)} %object_hbm.1, f32[3,2,256,256]{3,2,1,0:T(8,128)} %probe_hbm.1, bf16[6,256,256]{2,1,0:T(8,128)(2,1)} %raw_hbm.1, f32[256,256]{1,0:T(8,128)} %delta_hbm.1, ...), custom_call_target="tpu_custom_call" | custom-call | tf_op jit(solution)/shard_map/whole/pallas_call | solution.py:817
  75.1 3.1 %finish.1 = (f32[2,512,512]{2,1,0:T(8,128)}, f32[3,512,256]{2,1,0:T(8,128)}) custom-call(f32[2,512,512]{2,1,0:T(8,128)} %get-tuple-element.6.folded_in, f32[3,512,256]{2,1,0:T(8,128)} %get-tuple-element.7.summed_in), custom_call_target="tpu_custom_call" | custom-call | tf_op jit(solution)/shard_map/finish/pallas_call | solution.py:907
